TPU v7x, 32 devices: a whole 2x2x4 slice. The times are simulated.
32 devices in a mesh: gx: 4 (over y, x), gy: 4 (over z), gz: 2 (over core).
Axes of the slice: x: 2, y: 2, z: 4, core: 2. Of those that a mesh axis runs over, the one named last changes fastest.
Arguments:
- coords: float32 [4, 4, 6, 3, 128], P('gx', 'gy', 'gz'), as said below
- polar: float32 [4, 4, 6, 128], P('gx', 'gy', 'gz'), may hold values from 0.3 to 1.2
- field: float32 [4, 4, 6, 6, 128], P('gx', 'gy', 'gz'), may hold values from -6 to 6
- atom_count: int32 [4, 4, 6], P('gx', 'gy', 'gz'), may hold values from 64 to 128, as said below
- pair_list: int32 [4, 4, 6, 13], P('gx', 'gy', 'gz'), may hold values from -1 to 26, as said below
Outputs:
- dipoles: float32 [4, 4, 6, 6, 128], P('gx', 'gy', 'gz')
- residual: float32 [4, 4, 6, 6, 128], P('gx', 'gy', 'gz')
Inputs may be any that keep to these rules, and one draw needn't show every extreme that they name: `coords`: each coordinate lies within a quarter of 2.2 of its lattice site: atom slot a sits at 2.2 (a % 4 + 0.5, (a // 4) % 4 + 0.5, a // 16 + 0.5). `atom_count`: some block holds 128 atoms. `pair_list`: each block's row holds distinct codes above 13 in ascending order, followed by -1 in the unused entries.
All inputs are finite; a program needn't handle non-finite values.
Results may differ from a plain program's by a relative error of at most 0.0003.
Values sent between devices are 32-bit elements; how exact they have to be, the bound alone decides.
A program may use at most 64 MiB of HBM per device.

v0:
```python
import functools

import jax
import jax.numpy as jnp
from jax import lax
from jax.experimental import pallas as pl
from jax.experimental.pallas import tpu as pltpu
from jax.sharding import PartitionSpec as P

ITERS = 2


spacing = 2.2
cutoff_square = 49.0
thole = 0.39
chunk = 16


def extended(cells, sides, width):
    for axis, dim in sides:
        count = lax.axis_size(axis)
        head = lax.slice_in_dim(cells, 0, width, axis=dim)
        tail = lax.slice_in_dim(cells, cells.shape[dim] - width, cells.shape[dim], axis=dim)
        cells = jnp.concatenate(
            [
                lax.ppermute(tail, axis, [(i, (i + 1) % count) for i in range(count)]),
                cells,
                lax.ppermute(head, axis, [((i + 1) % count, i) for i in range(count)]),
            ],
            axis=dim,
        )
    return cells


def operator_kernel(blocks, box_size, flags_ref, geo_ref, vec_ref, out_ref, own_ref, acc_ref):
    block_x, block_y, block_z = blocks
    ext_y, ext_z = block_y + 2, block_z + 2
    slots = geo_ref.shape[-1]
    ones = jnp.ones((8, slots), jnp.float32)

    def pair(near, offset, is_self):
        rows = geo_ref[near]
        near_x = rows[0:1] + offset[0]
        near_y = rows[1:2] + offset[1]
        near_z = rows[2:3] + offset[2]
        near_p = thole * lax.rsqrt(rows[3:4])
        vec = vec_ref[near] * rows[4:5]
        for start in range(0, slots, chunk):
            span = pl.ds(start, chunk)
            dx = near_x - own_ref[0, span, :]
            dy = near_y - own_ref[1, span, :]
            dz = near_z - own_ref[2, span, :]
            square = dx * dx + dy * dy + dz * dz
            if is_self:
                row_id = lax.broadcasted_iota(jnp.int32, (chunk, slots), 0) + start
                col_id = lax.broadcasted_iota(jnp.int32, (chunk, slots), 1)
                same = row_id == col_id
                square = jnp.where(same, 1.0, square)
            inverse = lax.rsqrt(square)
            inverse_square = inverse * inverse
            damp = square * square * inverse * (near_p * own_ref[3, span, :])
            damping = jnp.exp(-damp)
            switch = jnp.maximum(1.0 - square * (1.0 / cutoff_square), 0.0)
            scale = switch * switch * (inverse_square * inverse)
            weight_three = scale * (1.0 - damping)
            weight_five = (1.0 - (1.0 + damp) * damping) * scale * (3.0 * inverse_square)
            if is_self:
                weight_three = jnp.where(same, 0.0, weight_three)
                weight_five = jnp.where(same, 0.0, weight_five)
            for dipole_set in range(2):
                vx = vec[3 * dipole_set : 3 * dipole_set + 1]
                vy = vec[3 * dipole_set + 1 : 3 * dipole_set + 2]
                vz = vec[3 * dipole_set + 2 : 3 * dipole_set + 3]
                along = (dx * vx + dy * vy + dz * vz) * weight_five
                acc_ref[3 * dipole_set, span, :] += dx * along - weight_three * vx
                acc_ref[3 * dipole_set + 1, span, :] += dy * along - weight_three * vy
                acc_ref[3 * dipole_set + 2, span, :] += dz * along - weight_three * vz

    @pl.loop(0, block_x * block_y * block_z)
    def _(block_id):
        place_x = block_id // (block_y * block_z) + 1
        place_y = block_id // block_z % block_y + 1
        place_z = block_id % block_z + 1
        own = (place_x * ext_y + place_y) * ext_z + place_z
        rows = geo_ref[own]
        for part in range(4):
            row = rows[part : part + 1]
            if part == 3:
                row = lax.rsqrt(row)
            own_ref[part] = jnp.broadcast_to(row, (slots, slots)).T
        acc_ref[...] = jnp.zeros_like(acc_ref)
        pair(own, (0.0, 0.0, 0.0), True)

        @pl.loop(0, 27)
        def _(code):
            off_x, off_y, off_z = code // 9 - 1, code // 3 % 3 - 1, code % 3 - 1
            near = own + (off_x * ext_y + off_y) * ext_z + off_z
            forward = flags_ref[own, code]
            backward = flags_ref[near, 26 - code]
            active = jnp.where(code > 13, forward, jnp.where(code < 13, backward, 0))

            @pl.when(active > 0)
            def _():
                offset = (
                    off_x.astype(jnp.float32) * box_size[0],
                    off_y.astype(jnp.float32) * box_size[1],
                    off_z.astype(jnp.float32) * box_size[2],
                )
                pair(near, offset, False)

        mask = rows[4:5]
        polar = rows[3:4]
        for part in range(6):
            total = lax.dot_general(
                ones,
                acc_ref[part],
                (((1,), (1,)), ((), ())),
                precision=lax.Precision.HIGHEST,
                preferred_element_type=jnp.float32,
            )
            vec_row = vec_ref[own, pl.ds(part, 1), :]
            out_ref[block_id, pl.ds(part, 1), :] = vec_row / polar - mask * total[0:1]


def set_sums(former, latter):
    product = (former * latter).reshape(former.shape[0:3] + (2, 3, former.shape[-1]))
    return jnp.sum(product, axis=(0, 1, 2, 4, 5))


def spread(values):
    return jnp.repeat(values, 3)[:, None]


def global_pair(residual, precond, operated):
    both = jnp.concatenate([set_sums(residual, precond), set_sums(precond, operated)])
    both = lax.psum(both, ("gx", "gy", "gz"))
    return both[0:2], both[2:4]


def on_device(coords, polar, field, atom_count, pair_list):
    blocks = coords.shape[0:3]
    block_x, block_y, block_z = blocks
    slots = coords.shape[-1]
    sides = (("gz", 2), ("gy", 1), ("gx", 0))
    slot_ids = jnp.arange(slots, dtype=jnp.int32)
    atom_mask = (slot_ids < atom_count[..., None]).astype(jnp.float32)[..., None, :]
    forward = jnp.any(pair_list[..., :, None] == slot_ids, axis=-2).astype(jnp.float32)
    polar_col = polar[..., None, :]
    source = field * atom_mask
    dipoles = polar_col * source
    packed = jnp.concatenate(
        [coords, polar_col, atom_mask, dipoles, forward[..., None, :]], axis=3
    )
    packed_ext = extended(packed, sides, 1).reshape(-1, 12, slots)
    flags = packed_ext[:, 11, :].astype(jnp.int32)
    geo_ext = packed_ext[:, 0:8]
    box_size = (4.0 * spacing, 4.0 * spacing, spacing * (slots // 16))
    total = block_x * block_y * block_z
    vmem = pl.BlockSpec(memory_space=pltpu.VMEM)
    apply_kernel = pl.pallas_call(
        functools.partial(operator_kernel, blocks, box_size),
        out_shape=jax.ShapeDtypeStruct((total, 6, slots), jnp.float32),
        in_specs=[pl.BlockSpec(memory_space=pltpu.SMEM), vmem, vmem],
        out_specs=vmem,
        scratch_shapes=[
            pltpu.VMEM((4, slots, slots), jnp.float32),
            pltpu.VMEM((6, slots, slots), jnp.float32),
        ],
    )

    def operator_ext(vector_ext):
        return apply_kernel(flags, geo_ext, vector_ext).reshape(dipoles.shape)

    def operator(vector):
        return operator_ext(extended(vector, sides, 1).reshape(-1, 6, slots))

    residual = source - operator_ext(packed_ext[:, 5:11])
    precond = polar_col * residual
    operated = operator(precond)
    norm_now, curve = global_pair(residual, precond, operated)
    step_len = norm_now / curve
    direction = precond
    projected = operated
    for iteration in range(ITERS):
        dipoles = dipoles + spread(step_len) * direction
        residual = residual - spread(step_len) * projected
        if iteration + 1 < ITERS:
            precond = polar_col * residual
            operated = operator(precond)
            norm_next, curve = global_pair(residual, precond, operated)
            conj_ratio = norm_next / norm_now
            step_len = norm_next / (curve - conj_ratio * norm_next / step_len)
            direction = precond + spread(conj_ratio) * direction
            projected = operated + spread(conj_ratio) * projected
            norm_now = norm_next
    return (dipoles, residual)


def solution(mesh):
    return jax.shard_map(
        on_device,
        mesh=mesh,
        in_specs=(
            P("gx", "gy", "gz", None, None),
            P("gx", "gy", "gz", None),
            P("gx", "gy", "gz", None, None),
            P("gx", "gy", "gz"),
            P("gx", "gy", "gz", None),
        ),
        out_specs=(P("gx", "gy", "gz", None, None), P("gx", "gy", "gz", None, None)),
        check_vma=False,
    )
```

profile of v0, /device:TPU:0, one launch (start us, length us, event | category | flops | bytes accessed | tf_op | source)
XLA Modules:
  0.0 184.0 jit_solution(8375020366116894012)
XLA Ops:
  5.4 2.7 %collective-permute-start.2 = (f32[1,1,5,12,128]{4,3,2,1,0:T(8,128)S(1)}, f32[1,1,5,12,128]{4,3,2,1,0:T(8,128)S(1)}, u32[]{:S(2)}, u32[]{:S(2)}) collective-permute-start(f32[1,1,5,12,128]{4,3,2,1,0:T(8,128)S(1)} %pad_maximum_fusion.6), channel_id=1, source_target_pairs={{0,2},{2,4},{4,6},{6,0},{1,3},{3,5},{5,7},{7,1},{8,10},{10,12},{12... | collective-permute-start | bytes 92168 | tf_op jit(solution)/shard_map/ppermute | solution.py:26
  8.1 2.1 %collective-permute-start.3 = (f32[1,1,5,12,128]{4,3,2,1,0:T(8,128)S(1)}, f32[1,1,5,12,128]{4,3,2,1,0:T(8,128)S(1)}, u32[]{:S(2)}, u32[]{:S(2)}) collective-permute-start(f32[1,1,5,12,128]{4,3,2,1,0:T(8,128)S(1)} %pad_maximum_fusion.6), channel_id=1, source_target_pairs={{2,0},{4,2},{6,4},{0,6},{3,1},{5,3},{7,5},{1,7},{10,8},{12,10},{14... | collective-permute-start | bytes 92168 | tf_op jit(solution)/shard_map/ppermute | solution.py:28
  10.2 2.1 %collective-permute-done.2 = f32[1,1,5,12,128]{4,3,2,1,0:T(8,128)S(1)} collective-permute-done((f32[1,1,5,12,128]{4,3,2,1,0:T(8,128)S(1)}, f32[1,1,5,12,128]{4,3,2,1,0:T(8,128)S(1)}, u32[]{:S(2)}, u32[]{:S(2)}) %collective-permute-start.2) | collective-permute-done | bytes 30752 | tf_op jit(solution)/shard_map/ppermute | solution.py:26
  12.7 1.5 collective-permute-start.4
  14.2 1.4 collective-permute-start.5
  15.6 3.8 %collective-permute-done.4 = f32[1,3,5,12,128]{4,3,2,1,0:T(8,128)S(1)} collective-permute-done((f32[1,3,5,12,128]{4,3,2,1,0:T(8,128)S(1)}, f32[1,3,5,12,128]{4,3,2,1,0:T(8,128)S(1)}, u32[]{:S(2)}, u32[]{:S(2)}) %collective-permute-start.4) | collective-permute-done | bytes 92192 | tf_op jit(solution)/shard_map/ppermute | solution.py:26
  19.5 1.0 collective-permute-done.5
  22.6 13.6 %shard_map.68 = f32[3,6,128]{2,1,0:T(8,128)} custom-call(s32[45,128]{1,0:T(8,128)} %bitcast.35, f32[45,8,128]{2,1,0:T(8,128)} %slice.55.geo_ref, f32[45,6,128]{2,1,0:T(8,128)} %slice.56.vec_ref), custom_call_target="tpu_custom_call" | custom-call | tf_op jit(solution)/shard_map/pallas_call | solution.py:172
  38.2 1.3 collective-permute-start.8
  39.5 3.3 %collective-permute-start.9 = (f32[1,1,5,6,128]{4,3,2,1,0:T(8,128)S(1)}, f32[1,1,5,6,128]{4,3,2,1,0:T(8,128)S(1)}, u32[]{:S(2)}, u32[]{:S(2)}) collective-permute-start(f32[1,1,5,6,128]{4,3,2,1,0:T(8,128)S(1)} %pad_maximum_fusion.7), channel_id=1, source_target_pairs={{2,0},{4,2},{6,4},{0,6},{3,1},{5,3},{7,5},{1,7},{10,8},{12,10},{14... | collective-permute-start | bytes 46088 | tf_op jit(solution)/shard_map/ppermute | solution.py:28
  42.8 1.8 collective-permute-done.8
  44.7 3.9 %collective-permute-start.11 = (f32[1,3,5,6,128]{4,3,2,1,0:T(8,128)S(1)}, f32[1,3,5,6,128]{4,3,2,1,0:T(8,128)S(1)}, u32[]{:S(2)}, u32[]{:S(2)}) collective-permute-start(f32[1,3,5,6,128]{4,3,2,1,0:T(8,128)S(1)} %pad_maximum_fusion.4), channel_id=1, source_target_pairs={{8,0},{16,8},{24,16},{0,24},{9,1},{17,9},{25,17},{1,25},{10,2},{18... | collective-permute-start | bytes 138248 | tf_op jit(solution)/shard_map/ppermute | solution.py:28
  48.6 2.8 %collective-permute-done.10 = f32[1,3,5,6,128]{4,3,2,1,0:T(8,128)S(1)} collective-permute-done((f32[1,3,5,6,128]{4,3,2,1,0:T(8,128)S(1)}, f32[1,3,5,6,128]{4,3,2,1,0:T(8,128)S(1)}, u32[]{:S(2)}, u32[]{:S(2)}) %collective-permute-start.10) | collective-permute-done | bytes 46112 | tf_op jit(solution)/shard_map/ppermute | solution.py:26
  52.1 13.6 %shard_map.69 = f32[3,6,128]{2,1,0:T(8,128)} custom-call(s32[45,128]{1,0:T(8,128)} %bitcast.36, f32[45,8,128]{2,1,0:T(8,128)} %slice.55.geo_ref, f32[45,6,128]{2,1,0:T(8,128)} %bitcast.34), custom_call_target="tpu_custom_call" | custom-call | tf_op jit(solution)/shard_map/pallas_call | solution.py:172
  67.0 43.4 %psum.14 = f32[4]{0:T(128)S(1)} all-reduce(f32[4]{0:T(128)S(1)} %pad_maximum_fusion.9), channel_id=1, replica_groups=mesh['gx'=4,'gy'=4,'gz'=2] {'gx','gy','gz'}, use_global_device_ids=true, to_apply=%region_5.0 | all-reduce | flops 4 | bytes 32 | tf_op jit(solution)/shard_map/psum | solution.py:136
  112.1 1.7 collective-permute-start.14
  113.8 2.1 %collective-permute-start.15 = (f32[1,1,5,6,128]{4,3,2,1,0:T(8,128)S(1)}, f32[1,1,5,6,128]{4,3,2,1,0:T(8,128)S(1)}, u32[]{:S(2)}, u32[]{:S(2)}) collective-permute-start(f32[1,1,5,6,128]{4,3,2,1,0:T(8,128)S(1)} %pad_maximum_fusion.8), channel_id=1, source_target_pairs={{2,0},{4,2},{6,4},{0,6},{3,1},{5,3},{7,5},{1,7},{10,8},{12,10},{14... | collective-permute-start | bytes 46088 | tf_op jit(solution)/shard_map/ppermute | solution.py:28
  115.9 1.9 %collective-permute-done.14 = f32[1,1,5,6,128]{4,3,2,1,0:T(8,128)S(1)} collective-permute-done((f32[1,1,5,6,128]{4,3,2,1,0:T(8,128)S(1)}, f32[1,1,5,6,128]{4,3,2,1,0:T(8,128)S(1)}, u32[]{:S(2)}, u32[]{:S(2)}) %collective-permute-start.14) | collective-permute-done | bytes 15392 | tf_op jit(solution)/shard_map/ppermute | solution.py:26
  117.8 2.3 %collective-permute-start.16 = (f32[1,3,5,6,128]{4,3,2,1,0:T(8,128)S(1)}, f32[1,3,5,6,128]{4,3,2,1,0:T(8,128)S(1)}, u32[]{:S(2)}, u32[]{:S(2)}) collective-permute-start(f32[1,3,5,6,128]{4,3,2,1,0:T(8,128)S(1)} %pad_maximum_fusion.5), channel_id=1, source_target_pairs={{0,8},{8,16},{16,24},{24,0},{1,9},{9,17},{17,25},{25,1},{2,10},{10... | collective-permute-start | bytes 138248 | tf_op jit(solution)/shard_map/ppermute | solution.py:26
  120.8 2.2 %collective-permute-done.16 = f32[1,3,5,6,128]{4,3,2,1,0:T(8,128)S(1)} collective-permute-done((f32[1,3,5,6,128]{4,3,2,1,0:T(8,128)S(1)}, f32[1,3,5,6,128]{4,3,2,1,0:T(8,128)S(1)}, u32[]{:S(2)}, u32[]{:S(2)}) %collective-permute-start.16) | collective-permute-done | bytes 46112 | tf_op jit(solution)/shard_map/ppermute | solution.py:26
  123.0 1.5 collective-permute-done.17
  125.2 13.6 %shard_map.70 = f32[3,6,128]{2,1,0:T(8,128)} custom-call(s32[45,128]{1,0:T(8,128)} %bitcast.37, f32[45,8,128]{2,1,0:T(8,128)} %slice.55.geo_ref, f32[45,6,128]{2,1,0:T(8,128)} %bitcast.33), custom_call_target="tpu_custom_call" | custom-call | tf_op jit(solution)/shard_map/pallas_call | solution.py:172
  138.8 0.9 multiply_reduce_fusion
  140.1 42.2 %psum.15 = f32[4]{0:T(128)S(1)} all-reduce(f32[4]{0:T(128)S(1)} %pad_maximum_fusion.10), channel_id=1, replica_groups=mesh['gx'=4,'gy'=4,'gz'=2] {'gx','gy','gz'}, use_global_device_ids=true, to_apply=%region_10.11 | all-reduce | flops 4 | bytes 32 | tf_op jit(solution)/shard_map/psum | solution.py:136
  (80 shorter events, 16.5 us)
Async XLA Ops:
  0.6 1.5 copy-start.4
  1.4 0.7 copy-start.3
  2.1 0.7 copy-start.5
  2.8 0.7 copy-start.2
  3.6 1.4 collective-permute-start
  4.2 1.2 collective-permute-start.1
  5.4 6.9 %collective-permute-start.2 = (f32[1,1,5,12,128]{4,3,2,1,0:T(8,128)S(1)}, f32[1,1,5,12,128]{4,3,2,1,0:T(8,128)S(1)}, u32[]{:S(2)}, u32[]{:S(2)}) collective-permute-start(f32[1,1,5,12,128]{4,3,2,1,0:T(8,128)S(1)} %pad_maximum_fusion.6), channel_id=1, source_target_pairs={{0,2},{2,4},{4,6},{6,0},{1,3},{3,5},{5,7},{7,1},{8,10},{10,12},{12... | collective-permute-start | bytes 92168 | tf_op jit(solution)/shard_map/ppermute | solution.py:26
  8.1 4.5 %collective-permute-start.3 = (f32[1,1,5,12,128]{4,3,2,1,0:T(8,128)S(1)}, f32[1,1,5,12,128]{4,3,2,1,0:T(8,128)S(1)}, u32[]{:S(2)}, u32[]{:S(2)}) collective-permute-start(f32[1,1,5,12,128]{4,3,2,1,0:T(8,128)S(1)} %pad_maximum_fusion.6), channel_id=1, source_target_pairs={{2,0},{4,2},{6,4},{0,6},{3,1},{5,3},{7,5},{1,7},{10,8},{12,10},{14... | collective-permute-start | bytes 92168 | tf_op jit(solution)/shard_map/ppermute | solution.py:28
  12.7 6.8 %collective-permute-start.4 = (f32[1,3,5,12,128]{4,3,2,1,0:T(8,128)S(1)}, f32[1,3,5,12,128]{4,3,2,1,0:T(8,128)S(1)}, u32[]{:S(2)}, u32[]{:S(2)}) collective-permute-start(f32[1,3,5,12,128]{4,3,2,1,0:T(8,128)S(1)} %pad_maximum_fusion.3), channel_id=1, source_target_pairs={{0,8},{8,16},{16,24},{24,0},{1,9},{9,17},{17,25},{25,1},{2,10},{10... | collective-permute-start | bytes 276488 | tf_op jit(solution)/shard_map/ppermute | solution.py:26
  14.2 6.3 %collective-permute-start.5 = (f32[1,3,5,12,128]{4,3,2,1,0:T(8,128)S(1)}, f32[1,3,5,12,128]{4,3,2,1,0:T(8,128)S(1)}, u32[]{:S(2)}, u32[]{:S(2)}) collective-permute-start(f32[1,3,5,12,128]{4,3,2,1,0:T(8,128)S(1)} %pad_maximum_fusion.3), channel_id=1, source_target_pairs={{8,0},{16,8},{24,16},{0,24},{9,1},{17,9},{25,17},{1,25},{10,2},{18... | collective-permute-start | bytes 276488 | tf_op jit(solution)/shard_map/ppermute | solution.py:28
  36.9 1.2 collective-permute-start.6
  36.9 1.3 collective-permute-start.7
  38.2 6.4 %collective-permute-start.8 = (f32[1,1,5,6,128]{4,3,2,1,0:T(8,128)S(1)}, f32[1,1,5,6,128]{4,3,2,1,0:T(8,128)S(1)}, u32[]{:S(2)}, u32[]{:S(2)}) collective-permute-start(f32[1,1,5,6,128]{4,3,2,1,0:T(8,128)S(1)} %pad_maximum_fusion.7), channel_id=1, source_target_pairs={{0,2},{2,4},{4,6},{6,0},{1,3},{3,5},{5,7},{7,1},{8,10},{10,12},{12... | collective-permute-start | bytes 46088 | tf_op jit(solution)/shard_map/ppermute | solution.py:26
  39.5 5.1 %collective-permute-start.9 = (f32[1,1,5,6,128]{4,3,2,1,0:T(8,128)S(1)}, f32[1,1,5,6,128]{4,3,2,1,0:T(8,128)S(1)}, u32[]{:S(2)}, u32[]{:S(2)}) collective-permute-start(f32[1,1,5,6,128]{4,3,2,1,0:T(8,128)S(1)} %pad_maximum_fusion.7), channel_id=1, source_target_pairs={{2,0},{4,2},{6,4},{0,6},{3,1},{5,3},{7,5},{1,7},{10,8},{12,10},{14... | collective-permute-start | bytes 46088 | tf_op jit(solution)/shard_map/ppermute | solution.py:28
  44.6 6.8 %collective-permute-start.10 = (f32[1,3,5,6,128]{4,3,2,1,0:T(8,128)S(1)}, f32[1,3,5,6,128]{4,3,2,1,0:T(8,128)S(1)}, u32[]{:S(2)}, u32[]{:S(2)}) collective-permute-start(f32[1,3,5,6,128]{4,3,2,1,0:T(8,128)S(1)} %pad_maximum_fusion.4), channel_id=1, source_target_pairs={{0,8},{8,16},{16,24},{24,0},{1,9},{9,17},{17,25},{25,1},{2,10},{10... | collective-permute-start | bytes 138248 | tf_op jit(solution)/shard_map/ppermute | solution.py:26
  44.7 6.7 %collective-permute-start.11 = (f32[1,3,5,6,128]{4,3,2,1,0:T(8,128)S(1)}, f32[1,3,5,6,128]{4,3,2,1,0:T(8,128)S(1)}, u32[]{:S(2)}, u32[]{:S(2)}) collective-permute-start(f32[1,3,5,6,128]{4,3,2,1,0:T(8,128)S(1)} %pad_maximum_fusion.4), channel_id=1, source_target_pairs={{8,0},{16,8},{24,16},{0,24},{9,1},{17,9},{25,17},{1,25},{10,2},{18... | collective-permute-start | bytes 138248 | tf_op jit(solution)/shard_map/ppermute | solution.py:28
  66.5 44.1 %copy-start = (f32[3,6,128]{2,1,0:T(8,128)S(1)}, f32[3,6,128]{2,1,0:T(8,128)}, u32[]{:S(2)}) copy-start(f32[3,6,128]{2,1,0:T(8,128)} %shard_map.69) | copy-start | bytes 27652
  110.7 1.2 collective-permute-start.12
  110.8 1.3 collective-permute-start.13
  112.1 5.7 %collective-permute-start.14 = (f32[1,1,5,6,128]{4,3,2,1,0:T(8,128)S(1)}, f32[1,1,5,6,128]{4,3,2,1,0:T(8,128)S(1)}, u32[]{:S(2)}, u32[]{:S(2)}) collective-permute-start(f32[1,1,5,6,128]{4,3,2,1,0:T(8,128)S(1)} %pad_maximum_fusion.8), channel_id=1, source_target_pairs={{0,2},{2,4},{4,6},{6,0},{1,3},{3,5},{5,7},{7,1},{8,10},{10,12},{12... | collective-permute-start | bytes 46088 | tf_op jit(solution)/shard_map/ppermute | solution.py:26
  113.8 4.0 %collective-permute-start.15 = (f32[1,1,5,6,128]{4,3,2,1,0:T(8,128)S(1)}, f32[1,1,5,6,128]{4,3,2,1,0:T(8,128)S(1)}, u32[]{:S(2)}, u32[]{:S(2)}) collective-permute-start(f32[1,1,5,6,128]{4,3,2,1,0:T(8,128)S(1)} %pad_maximum_fusion.8), channel_id=1, source_target_pairs={{2,0},{4,2},{6,4},{0,6},{3,1},{5,3},{7,5},{1,7},{10,8},{12,10},{14... | collective-permute-start | bytes 46088 | tf_op jit(solution)/shard_map/ppermute | solution.py:28
  117.8 5.2 %collective-permute-start.16 = (f32[1,3,5,6,128]{4,3,2,1,0:T(8,128)S(1)}, f32[1,3,5,6,128]{4,3,2,1,0:T(8,128)S(1)}, u32[]{:S(2)}, u32[]{:S(2)}) collective-permute-start(f32[1,3,5,6,128]{4,3,2,1,0:T(8,128)S(1)} %pad_maximum_fusion.5), channel_id=1, source_target_pairs={{0,8},{8,16},{16,24},{24,0},{1,9},{9,17},{17,25},{25,1},{2,10},{10... | collective-permute-start | bytes 138248 | tf_op jit(solution)/shard_map/ppermute | solution.py:26
  120.1 4.3 %collective-permute-start.17 = (f32[1,3,5,6,128]{4,3,2,1,0:T(8,128)S(1)}, f32[1,3,5,6,128]{4,3,2,1,0:T(8,128)S(1)}, u32[]{:S(2)}, u32[]{:S(2)}) collective-permute-start(f32[1,3,5,6,128]{4,3,2,1,0:T(8,128)S(1)} %pad_maximum_fusion.5), channel_id=1, source_target_pairs={{8,0},{16,8},{24,16},{0,24},{9,1},{17,9},{25,17},{1,25},{10,2},{18... | collective-permute-start | bytes 138248 | tf_op jit(solution)/shard_map/ppermute | solution.py:28
  139.8 42.9 %copy-start.1 = (f32[3,6,128]{2,1,0:T(8,128)S(1)}, f32[3,6,128]{2,1,0:T(8,128)}, u32[]{:S(2)}) copy-start(f32[3,6,128]{2,1,0:T(8,128)} %shard_map.70) | copy-start | bytes 27652
where the time goes:
time: 183 us; the launch traced here: 184 us
  blocking collectives  85.6 us (47%)
  Pallas kernels  40.8 us (22%)
  starting transfers between devices  24.8 us (14%)
  waiting for transfers between devices  20.2 us (11%)
  other arithmetic  6.43 us (4%)
  local copies, waits for them, and re-layouts  5.45 us (3%)
    psum x2, blocking collectives, global_pair(): both = lax.psum(both, ('gx', 'gy', 'gz'))  85.6 us
    pallas_call x3, Pallas kernels, operator_ext(): return apply_kernel(flags, geo_ext, vector_ext).reshape(dipoles.shape)  40.8 us
    ppermute x9, waiting for transfers between devices, extended(): lax.ppermute(tail, axis, [(i, (i + 1) % count) for i in range(count)])  16.6 us
    ppermute x9, starting transfers between devices, extended(): lax.ppermute(head, axis, [((i + 1) % count, i) for i in range(count)])  14.6 us
    ppermute x9, starting transfers between devices, extended(): lax.ppermute(tail, axis, [(i, (i + 1) % count) for i in range(count)])  10.2 us
  transfers between devices with their start and end apart: 18, of which 15 were waited for; matrix products, arithmetic and copies ran while one was open for 0% of the time, Pallas kernels for 0%

commit v1 on v0

v1 whole, which is shorter than its diff:
```python
import functools

import jax
import jax.numpy as jnp
from jax import lax
from jax.experimental import pallas as pl
from jax.experimental.pallas import tpu as pltpu
from jax.sharding import PartitionSpec as P

MESH = pl.DeviceIdType.MESH
AXES = ("gx", "gy", "gz")
spacing = 2.2
cutoff_square = 49.0
thole = 0.39
SIDE = 4
GROUP = SIDE * SIDE
REACH = 3
SHIFTS = 2 * REACH + 1
COLUMNS = [(cx, cy) for cx in (-1, 0, 1) for cy in (-1, 0, 1)]
CENTRE = COLUMNS.index((0, 0))
SIDES = [index for index in range(9) if index != CENTRE]


def gather(value, index):
    return jnp.take_along_axis(value, index, axis=1, mode="promise_in_bounds")


def kernel(
    sizes, deep, pairs_ref, count_ref, coords_ref, polar_ref, field_ref, dip_out, res_out,
    send_dip, send_geo, main_dip, above_dip, below_dip, main_geo, above_geo, below_geo,
    near, near_geo, switch, tensor, sums_out, sums_in, send_sems, recv_sems, geo_send, geo_recv,
    sum_send, sum_recv,
):
    total_devices = sizes[0] * sizes[1] * sizes[2]
    me = [lax.axis_index(name) for name in AXES]
    my_id = (me[0] * sizes[1] + me[1]) * sizes[2] + me[2]

    def device_at(linear):
        return (
            linear // (sizes[1] * sizes[2]),
            linear // sizes[2] % sizes[1],
            linear % sizes[2],
        )

    def neighbour(cx, cy, cz):
        return tuple(
            lax.rem(place + step + size, size)
            for place, step, size in zip(me, (cx, cy, cz), sizes)
        )

    barrier = pltpu.get_barrier_semaphore()
    for step in range(1, total_devices):
        other = lax.rem(my_id + step, total_devices)
        pl.semaphore_signal(barrier, inc=1, device_id=device_at(other), device_id_type=MESH)

    lane = lax.broadcasted_iota(jnp.int32, (8, 128), 1)
    row = lax.broadcasted_iota(jnp.int32, (8, 128), 0)
    group = lane // GROUP
    place_y = lane // SIDE % SIDE
    place_x = lane % SIDE
    site = lane % GROUP
    shift_x = group - REACH
    unpack = GROUP * row + site

    def rows_of(line):
        return gather(jnp.broadcast_to(line, (8, 128)), unpack)

    site_x = spacing * (place_x.astype(jnp.float32) + 0.5)
    site_y = spacing * (place_y.astype(jnp.float32) + 0.5)
    site_z = spacing * (row.astype(jnp.float32) + 0.5)

    def packed(parts):
        value = parts[0]
        for index in range(1, len(parts)):
            value = jnp.where(group == index, parts[index], value)
        return value

    own, polar, mask, source, dipoles = [], [], [], [], []
    for k in range(deep):
        places = [
            rows_of(coords_ref[3 * k + part]) - offset
            for part, offset in enumerate((site_x, site_y, site_z))
        ]
        polar_k = rows_of(polar_ref[k])
        mask_k = jnp.where(unpack < count_ref[k], 1.0, 0.0)
        source_k = [rows_of(field_ref[6 * k + part]) * mask_k for part in range(6)]
        dipoles_k = [polar_k * value for value in source_k]
        root = lax.rsqrt(polar_k)
        slot = lane - 5 * GROUP + 14
        flag = pairs_ref[k, 0] == slot
        for entry in range(1, 13):
            flag = jnp.logical_or(flag, pairs_ref[k, entry] == slot)
        flags = jnp.where(flag, 1.0, 0.0)
        send_dip[0, pl.ds(8 * k, 8), :] = packed(dipoles_k)
        send_geo[pl.ds(8 * k, 8), :] = packed(places + [root, mask_k, flags])
        own.append(places + [thole * root])
        polar.append(polar_k)
        mask.append(mask_k)
        source.append(source_k)
        dipoles.append(dipoles_k)

    pl.semaphore_wait(barrier, total_devices - 1)

    def exchange(source_ref, main, above, below, send_sem, recv_sem):
        copies = []

        def send(src, dst, number, target):
            copy = pltpu.make_async_remote_copy(
                src_ref=src,
                dst_ref=dst,
                send_sem=send_sem.at[number],
                recv_sem=recv_sem.at[number],
                device_id=target,
                device_id_type=MESH,
            )
            copy.start()
            copies.append(copy)

        order = sorted(range(9), key=lambda index: -abs(COLUMNS[index][0]) - abs(COLUMNS[index][1]))
        for index in order:
            cx, cy = COLUMNS[index]
            there = COLUMNS.index((-cx, -cy))
            if index != CENTRE:
                send(source_ref, main.at[there], there, neighbour(cx, cy, 0))
            send(
                source_ref.at[pl.ds(0, 8)], above.at[there], 9 + there, neighbour(cx, cy, -1)
            )
            send(
                source_ref.at[pl.ds(8 * (deep - 1), 8)], below.at[there], 18 + there,
                neighbour(cx, cy, 1),
            )
        return copies

    def column_tiles(source_ref, main, above, below, index):
        halo = jnp.where(row < 4, above[index], below[index])
        tiles = [halo]
        for k in range(deep):
            if index == CENTRE:
                tiles.append(source_ref[pl.ds(8 * k, 8), :])
            else:
                tiles.append(main[index, pl.ds(8 * k, 8), :])
        return tiles

    reached_x = place_x + shift_x
    turn_x = [GROUP * part + SIDE * place_y + (reached_x & (SIDE - 1)) for part in range(6)]
    turn_y = [GROUP * group + SIDE * ((place_y + step) & (SIDE - 1)) + place_x for step in range(SIDE)]

    def spread_out(source_ref, main, above, below, out, parts):
        for part in range(parts):
            lined = {}
            for cy in (-1, 0, 1):
                columns = [
                    column_tiles(source_ref, main, above, below, COLUMNS.index((cx, cy)))
                    for cx in (-1, 0, 1)
                ]
                for v in range(deep + 1):
                    low, mid, high = (gather(columns[cx][v], turn_x[part]) for cx in range(3))
                    value = jnp.where(reached_x < 0, low, jnp.where(reached_x < SIDE, mid, high))
                    lined[cy, v] = value
            for number in range(SHIFTS):
                sy = number - REACH
                for v in range(deep + 1):
                    value = lined[0, v]
                    if sy > 0:
                        value = jnp.where(place_y < sy, lined[1, v], value)
                    if sy < 0:
                        value = jnp.where(place_y >= SIDE + sy, lined[-1, v], value)
                    if sy != 0:
                        value = gather(value, turn_y[sy % SIDE])
                    out[number, part, pl.ds(8 * v, 8), :] = value
                    if v == 0:
                        out[number, part, pl.ds(8 * (deep + 1), 8), :] = value

    def finish(sums, vector):
        result = []
        for k in range(deep):
            values = []
            for part in range(6):
                value = sums[k][part]
                for step in (64, 32, 16):
                    value = value + pltpu.roll(value, step, 1)
                values.append(vector[k][part] / polar[k] - mask[k] * value)
            result.append(values)
        return result

    def nest(flat):
        return [[flat[6 * k + part] for part in range(6)] for k in range(deep)]

    zeros = tuple(jnp.zeros((8, 128), jnp.float32) for _ in range(6 * deep))

    def contract(sums, k, parts, vec):
        xx, yy, zz, xy, xz, yz = parts
        for first in (0, 3):
            vx, vy, vz = vec[first : first + 3]
            base = 6 * k + first
            sums[base] = sums[base] + (xx * vx + xy * vy + xz * vz)
            sums[base + 1] = sums[base + 1] + (xy * vx + yy * vy + yz * vz)
            sums[base + 2] = sums[base + 2] + (xz * vx + yz * vy + zz * vz)

    def apply(vec_ref):
        def step(number, sums):
            sums = list(sums)
            for k in range(deep):
                for index in range(SHIFTS):
                    span = pl.ds(8 * k + 8 + index - REACH, 8)
                    parts = [tensor[number, k * SHIFTS + index, part] for part in range(6)]
                    vec = [vec_ref[number, part, span, :] for part in range(6)]
                    contract(sums, k, parts, vec)
            return tuple(sums)

        return nest(lax.fori_loop(0, SHIFTS, step, zeros))

    far_x = spacing * shift_x.astype(jnp.float32)

    def build(vec_ref):
        def step(number, sums):
            sums = list(sums)
            sy = number - REACH
            far_y = spacing * sy.astype(jnp.float32)
            is_self = jnp.logical_and(group == REACH, sy == 0)
            for k in range(deep):
                own_x = own[k][0] - far_x
                own_y = own[k][1] - far_y
                for index in range(SHIFTS):
                    start = 8 + index - REACH
                    span = pl.ds(8 * k + start, 8)
                    dx = near_geo[number, 0, span, :] - own_x
                    dy = near_geo[number, 1, span, :] - own_y
                    dz = near_geo[number, 2, span, :] - (own[k][2] - spacing * (index - REACH))
                    weight = switch[k, number, pl.ds(start, 8), :]
                    if index == REACH:
                        weight = jnp.where(is_self, 0.0, weight)
                    square = jnp.maximum(dx * dx + dy * dy + dz * dz, 1.0)
                    inverse = lax.rsqrt(square)
                    inverse_square = inverse * inverse
                    damp = square * square * inverse * (near_geo[number, 3, span, :] * own[k][3])
                    damping = jnp.exp(-damp)
                    fade = jnp.maximum(1.0 - square * (1.0 / cutoff_square), 0.0)
                    scale = fade * fade * (inverse_square * inverse) * weight
                    three = scale * (1.0 - damping)
                    five = (1.0 - (1.0 + damp) * damping) * scale * (3.0 * inverse_square)
                    tx, ty, tz = five * dx, five * dy, five * dz
                    parts = (
                        tx * dx - three, ty * dy - three, tz * dz - three, tx * dy, tx * dz, ty * dz
                    )
                    for part in range(6):
                        tensor[number, k * SHIFTS + index, part] = parts[part]
                    vec = [vec_ref[number, part, span, :] for part in range(6)]
                    contract(sums, k, parts, vec)
            return tuple(sums)

        return nest(lax.fori_loop(0, SHIFTS, step, zeros))

    def build_switch():
        def code_of(cx, cy, cz):
            return 9 * (cx + 1) + 3 * (cy + 1) + cz + 1

        def flag_lane(code):
            return 5 * GROUP + code - 14

        def pick(tile, at):
            return gather(tile, jnp.full((8, 128), at, jnp.int32))

        tiles = {
            index: column_tiles(send_geo, main_geo, above_geo, below_geo, index)
            for index in range(9)
            if COLUMNS[index] < (0, 1)
        }
        for k in range(deep):
            for cz in (-1, 0, 1):
                v = (k + 1 + cz) % (deep + 1)
                active = {}
                for cy in (-1, 0, 1):
                    sides = []
                    for cx in (-1, 0, 1):
                        code = code_of(cx, cy, cz)
                        if code == 13:
                            sides.append(jnp.ones((8, 128), jnp.float32))
                        elif code > 13:
                            sides.append(pick(tiles[CENTRE][k + 1], flag_lane(code)))
                        else:
                            near_tile = tiles[COLUMNS.index((cx, cy))][v]
                            sides.append(pick(near_tile, flag_lane(26 - code)))
                    value = jnp.where(
                        reached_x < 0, sides[0], jnp.where(reached_x < SIDE, sides[1], sides[2])
                    )
                    active[cy] = jnp.where(group < SHIFTS, value, 0.0)
                for number in range(SHIFTS):
                    sy = number - REACH
                    value = active[0]
                    if sy > 0:
                        value = jnp.where(place_y + sy >= SIDE, active[1], value)
                    if sy < 0:
                        value = jnp.where(place_y + sy < 0, active[-1], value)
                    row_mask = near_geo[number, 4, pl.ds(8 * (k + 1 + cz), 8), :]
                    switch[k, number, pl.ds(8 * (cz + 1), 8), :] = value * row_mask

    def partial(first, second, dipole_set):
        value = None
        for k in range(deep):
            for part in range(3 * dipole_set, 3 * dipole_set + 3):
                term = first[k][part] * second[k][part]
                value = term if value is None else value + term
        return value

    def start_sums(number, values):
        line = jnp.sum(packed(values), axis=0, keepdims=True)
        sums_out[number] = line
        sums_in[number, my_id] = line
        copies = []
        for step in range(1, total_devices):
            other = lax.rem(my_id + step, total_devices)
            copy = pltpu.make_async_remote_copy(
                src_ref=sums_out.at[number],
                dst_ref=sums_in.at[number, my_id],
                send_sem=sum_send.at[number, step],
                recv_sem=sum_recv.at[number, step],
                device_id=device_at(other),
                device_id_type=MESH,
            )
            copy.start()
            copies.append(copy)
        return copies

    def end_sums(number, copies, amount):
        for copy in copies:
            copy.wait_recv()
        lines = [sums_in[number, index] for index in range(total_devices)]
        while len(lines) > 1:
            lines = [
                lines[index] + lines[index + 1] if index + 1 < len(lines) else lines[index]
                for index in range(0, len(lines), 2)
            ]
        line = lines[0]
        line_group = lax.broadcasted_iota(jnp.int32, (1, 128), 1) // GROUP
        return [
            jnp.broadcast_to(
                jnp.sum(jnp.where(line_group == index, line, 0.0), axis=1, keepdims=True), (8, 128)
            )
            for index in range(amount)
        ]

    def each(function, *vectors):
        return [
            [function(k, part, *(vector[k][part] for vector in vectors)) for part in range(6)]
            for k in range(deep)
        ]

    started = []
    geo_copies = exchange(send_geo, main_geo, above_geo, below_geo, geo_send, geo_recv)
    started += geo_copies

    def vector_exchange(phase):
        refs = (send_dip.at[phase], main_dip.at[phase], above_dip.at[phase], below_dip.at[phase])
        copies = exchange(*refs, send_sems.at[phase], recv_sems.at[phase])
        started.extend(copies)
        return refs, copies

    def arrive(refs, copies):
        for copy in copies:
            copy.wait_recv()
        spread_out(*refs, near, 6)

    refs, copies = vector_exchange(0)
    for copy in geo_copies:
        copy.wait_recv()
    spread_out(send_geo, main_geo, above_geo, below_geo, near_geo, 5)
    build_switch()
    arrive(refs, copies)
    image = finish(build(near), dipoles)
    residual = each(lambda k, part, s, a: s - a, source, image)
    precond = each(lambda k, part, r: polar[k] * r, residual)
    for k in range(deep):
        send_dip[1, pl.ds(8 * k, 8), :] = packed(precond[k])
    arrive(*vector_exchange(1))
    image = finish(apply(near), precond)
    turned = each(lambda k, part, q: polar[k] * q, image)
    for k in range(deep):
        send_dip[2, pl.ds(8 * k, 8), :] = packed(turned[k])
    refs, copies = vector_exchange(2)
    first_sums = start_sums(
        0,
        [partial(residual, precond, s) for s in range(2)]
        + [partial(precond, image, s) for s in range(2)],
    )
    started += first_sums
    arrive(refs, copies)
    turned_image = finish(apply(near), turned)
    totals = end_sums(0, first_sums, 4)
    norm, curve = totals[0:2], totals[2:4]
    gamma = [norm[s] / curve[s] for s in range(2)]
    dipoles = each(lambda k, part, d, p: d + gamma[part // 3] * p, dipoles, precond)
    residual = each(lambda k, part, r, q: r - gamma[part // 3] * q, residual, image)
    second = each(lambda k, part, r: polar[k] * r, residual)
    second_image = each(lambda k, part, q, t: q - gamma[part // 3] * t, image, turned_image)
    last_sums = start_sums(
        1,
        [partial(residual, second, s) for s in range(2)]
        + [partial(second, second_image, s) for s in range(2)]
        + [partial(second, image, s) for s in range(2)]
        + [partial(precond, second_image, s) for s in range(2)],
    )
    started += last_sums
    totals = end_sums(1, last_sums, 8)
    ratio = [totals[s] / norm[s] for s in range(2)]
    gamma = [
        totals[s]
        / (totals[2 + s] + ratio[s] * (totals[4 + s] + totals[6 + s] + ratio[s] * curve[s]))
        for s in range(2)
    ]
    for k in range(deep):
        for part in range(6):
            s = part // 3
            direction = second[k][part] + ratio[s] * precond[k][part]
            along = second_image[k][part] + ratio[s] * image[k][part]
            for out, value in (
                (dip_out, dipoles[k][part] + gamma[s] * direction),
                (res_out, residual[k][part] - gamma[s] * along),
            ):
                line = jnp.sum(jnp.where(group == row, value, 0.0), axis=0, keepdims=True)
                out[6 * k + part] = line
    for copy in started:
        copy.wait_send()


def on_device(sizes, coords, polar, field, atom_count, pair_list):
    deep, slots = coords.shape[2], coords.shape[-1]
    assert coords.shape[0:2] == (1, 1) and slots == 128
    vmem = pl.BlockSpec(memory_space=pltpu.VMEM)
    smem = pl.BlockSpec(memory_space=pltpu.SMEM)
    rows = 8 * deep
    total = sizes[0] * sizes[1] * sizes[2]

    def buffer(*shape):
        return pltpu.VMEM(shape, jnp.float32)

    line = jax.ShapeDtypeStruct((6 * deep, 1, slots), jnp.float32)
    dma = pltpu.SemaphoreType.DMA
    dipoles, residual = pl.pallas_call(
        functools.partial(kernel, sizes, deep),
        out_shape=(line, line),
        in_specs=[smem, smem, vmem, vmem, vmem],
        out_specs=(vmem, vmem),
        scratch_shapes=[
            buffer(3, rows, slots),
            buffer(rows, slots),
            buffer(3, 9, rows, slots),
            buffer(3, 9, 8, slots),
            buffer(3, 9, 8, slots),
            buffer(9, rows, slots),
            buffer(9, 8, slots),
            buffer(9, 8, slots),
            buffer(SHIFTS, 6, rows + 16, slots),
            buffer(SHIFTS, 5, rows + 16, slots),
            buffer(deep, SHIFTS, 24, slots),
            buffer(SHIFTS, SHIFTS * deep, 6, 8, slots),
            buffer(2, 1, slots),
            buffer(2, total, 1, slots),
            dma((3, 27)),
            dma((3, 27)),
            dma((27,)),
            dma((27,)),
            dma((2, total)),
            dma((2, total)),
        ],
        compiler_params=pltpu.CompilerParams(collective_id=0, has_side_effects=True),
    )(
        pair_list.reshape(deep, 13),
        atom_count.reshape(deep),
        coords.reshape(3 * deep, 1, slots),
        polar.reshape(deep, 1, slots),
        field.reshape(6 * deep, 1, slots),
    )
    return dipoles.reshape(field.shape), residual.reshape(field.shape)


def solution(mesh):
    sizes = tuple(mesh.shape[name] for name in AXES)
    block = P(*AXES, None, None)
    return jax.shard_map(
        functools.partial(on_device, sizes),
        mesh=mesh,
        in_specs=(block, P(*AXES, None), block, P(*AXES), P(*AXES, None)),
        out_specs=(block, block),
        check_vma=False,
    )
```

time: 183 us -> 46.1 us (0.25)
  blocking collectives: 85.6 us -> 0 us
  starting transfers between devices: 24.8 us -> 0 us
  waiting for transfers between devices: 20.2 us -> 0 us
  other arithmetic: 6.43 us -> 0 us
  local copies, waits for them, and re-layouts: 5.45 us -> 3.16 us
    psum x2 -> x0, blocking collectives: 85.6 us -> none  [global_pair(): both = lax.psum(both, ('gx', 'gy', 'gz'))]
    ppermute x18 -> x0, starting transfers between devices: 24.8 us -> none  [the longest x9 14.6 us: extended(): lax.ppermute(head, axis, [((i + 1) % count, i) for i in range(count)])]
    ppermute x18 -> x0, waiting for transfers between devices: 20.2 us -> none  [the longest x9 16.6 us: extended(): lax.ppermute(tail, axis, [(i, (i + 1) % count) for i in range(count)])]
    reduce_sum x6 -> x0, other arithmetic: 2.18 us -> none  [set_sums(): return jnp.sum(product, axis=(0, 1, 2, 4, 5))]
    pallas_call x3 -> x1, Pallas kernels: 40.8 us -> 42.1 us  [on_device(): pl.pallas_call(functools.partial(kernel, sizes, deep), out_shape=(line, l...]
  transfers between devices with their start and end apart: 18 -> 0, of which waited for: 15 -> 0; matrix products, arithmetic and copies ran while one was open for 0% -> 0% of each run, Pallas kernels for 0% -> 0%
where the time goes in v1:
time: 46.1 us; the launch traced here: 45.9 us
  Pallas kernels  42.1 us (91%)
  local copies, waits for them, and re-layouts  3.16 us (7%)
  between operations  0.66 us (1%)
    pallas_call x1, Pallas kernels, on_device(): pl.pallas_call(functools.partial(kernel, sizes, deep), out_shape=(line, l...  42.1 us
    unnamed x7, local copies, waits for them, and re-layouts  3.16 us

profile of v1, /device:TPU:0, one launch (start us, length us, event | category | flops | bytes accessed | tf_op | source)
XLA Modules:
  0.0 45.9 jit_solution(9398144892078929468)
XLA Ops:
  0.6 0.0 copy-start.1
  0.6 0.7 %copy-done.1 = s32[1,1,3,13]{3,1,2,0:T(1,128)S(1)} copy-done((s32[1,1,3,13]{3,1,2,0:T(1,128)S(1)}, s32[1,1,3,13]{3,1,2,0:T(1,128)}, u32[]{:S(2)}) %copy-start.1) | copy-done | bytes 180
  1.3 0.6 %copy.11 = s32[1,1,3,13]{3,2,1,0:T(4,128)} copy(s32[1,1,3,13]{3,1,2,0:T(1,128)S(1)} %copy-done.1) | data formatting | bytes 312
  1.9 42.1 %shard_map.68 = (f32[18,1,128]{2,1,0:T(1,128)}, f32[18,1,128]{2,1,0:T(1,128)}) custom-call(s32[3,13]{1,0:T(4,128)} %bitcast.16, s32[3]{0:T(128)} %bitcast.19, f32[9,1,128]{2,1,0:T(1,128)} %bitcast.17, f32[3,1,128]{2,1,0:T(1,128)} %bitcast.18, f32[18,1,128]{2,1,0:T(1,128)} %bitcast.13), custom_call_target="tpu_custom_call" | custom-call | tf_op jit(solution)/shard_map/pallas_call | solution.py:439
  44.0 0.0 copy-start
  44.0 1.3 %copy.14 = f32[1,1,3,6,128]{4,1,3,2,0:T(1,128)} copy(f32[1,1,3,6,128]{4,1,3,2,0:T(1,128)} %bitcast.15) | data formatting | bytes 18432
  45.3 0.0 copy-done
  45.3 0.6 %copy.15 = f32[1,1,3,6,128]{4,1,3,2,0:T(1,128)} copy(f32[1,1,3,6,128]{4,1,3,2,0:T(1,128)S(1)} %bitcast.14) | data formatting | bytes 18432
Async XLA Ops:
  0.6 0.7 %copy-start.1 = (s32[1,1,3,13]{3,1,2,0:T(1,128)S(1)}, s32[1,1,3,13]{3,1,2,0:T(1,128)}, u32[]{:S(2)}) copy-start(s32[1,1,3,13]{3,1,2,0:T(1,128)} %param.9) | copy-start | bytes 472
  44.0 1.3 %copy-start = (f32[18,1,128]{2,1,0:T(1,128)S(1)}, f32[18,1,128]{2,1,0:T(1,128)}, u32[]{:S(2)}) copy-start(f32[18,1,128]{2,1,0:T(1,128)} %get-tuple-element.5) | copy-start | bytes 27652

commit v2 on v0

v2 whole, which is shorter than its diff:
```python
import functools

import jax
import jax.numpy as jnp
from jax import lax
from jax.experimental import pallas as pl
from jax.experimental.pallas import tpu as pltpu
from jax.sharding import PartitionSpec as P

MESH = pl.DeviceIdType.MESH
AXES = ("gx", "gy", "gz")
spacing = 2.2
cutoff_square = 49.0
thole = 0.39
SIDE = 4
GROUP = SIDE * SIDE
REACH = 3
SHIFTS = range(-REACH, REACH + 1)
SPAN = 2 * REACH + 1
COLUMNS = [(cx, cy) for cx in (-1, 0, 1) for cy in (-1, 0, 1)]
EDGE = 12
OWN = (0, 48)
LOW = ((48, 60, 72), (36, 96, 108))
HIGH = ((84, 96, 108), (0, 12, 24))
RIDE_LOW = 0
RIDE_HIGH = 36
FLAGS = 4


def gather(value, index):
    return jnp.take_along_axis(value, index, axis=1, mode="promise_in_bounds")


def flag_slot(flag):
    return 4 * flag if flag < 4 else 4 * ((flag - 4) // 3) + 1 + (flag - 4) % 3


def plan(deep, rings):
    riders = [k for k in range(deep) if k % 3 == 2]
    tile_of, tiles = {}, 0
    for k in range(deep):
        if k not in riders:
            tile_of[k] = tiles
            tiles += 1
    slots, total = {}, 0
    for column in COLUMNS:
        if column != (0, 0):
            slots[column] = total
            total += tiles if column[0] else deep
    halos = {}
    for column in COLUMNS:
        halos[column] = total
        total += rings
    return riders, tile_of, tiles, slots, halos, total


def kernel(
    sizes, deep, pairs_hbm, count_hbm, coords_hbm, polar_hbm, field_hbm, dip_out, res_out,
    pairs_ref, count_ref, coords_ref, polar_ref, field_ref, send, held, near, near_geo, own_ref,
    switch, tensor, sums_out, sums_in, load_sems, send_sems, recv_sems, sum_send, sum_recv,
):
    total_devices = sizes[0] * sizes[1] * sizes[2]
    rings = 1 if sizes[2] == 2 else 2
    riders, tile_of, tiles, slots, halos, total_tiles = plan(deep, rings)
    me = [lax.axis_index(name) for name in AXES]
    my_id = (me[0] * sizes[1] + me[1]) * sizes[2] + me[2]
    scope = jax.named_scope

    def device_at(linear):
        return (
            linear // (sizes[1] * sizes[2]),
            linear // sizes[2] % sizes[1],
            linear % sizes[2],
        )

    def neighbour(cx, cy, cz):
        return tuple(
            lax.rem(place + step + size, size)
            for place, step, size in zip(me, (cx, cy, cz), sizes)
        )

    with scope("signal"):
        barrier = pltpu.get_barrier_semaphore()
        for step in range(1, total_devices):
            other = lax.rem(my_id + step, total_devices)
            pl.semaphore_signal(barrier, inc=1, device_id=device_at(other), device_id_type=MESH)
        loads = [
            pltpu.make_async_copy(src, dst, load_sems.at[index])
            for index, (src, dst) in enumerate(
                (
                    (pairs_hbm, pairs_ref),
                    (count_hbm, count_ref),
                    (coords_hbm, coords_ref),
                    (polar_hbm, polar_ref),
                    (field_hbm, field_ref),
                )
            )
        ]
        for copy in loads:
            copy.start()

    lane = lax.broadcasted_iota(jnp.int32, (8, 128), 1)
    row = lax.broadcasted_iota(jnp.int32, (8, 128), 0)
    group = lane // GROUP
    place_y = lane // SIDE % SIDE
    place_x = lane % SIDE
    site = lane % GROUP
    shift_x = group - REACH
    unpack = GROUP * row + site
    far_x = spacing * shift_x.astype(jnp.float32)

    def within(first, size):
        return jnp.logical_and(lane >= first, lane < first + size)

    def choose(cases, default):
        for condition, value in cases:
            default = jnp.where(condition, value, default)
        return default

    def edge_index(bases, at, first_x):
        cases = []
        for base, start in zip(bases, at):
            local = lane - base
            value = start + SIDE * (local // 3) + local % 3 + first_x
            cases.append((within(base, EDGE), value))
        return choose(cases, jnp.zeros_like(lane))

    all_parts = [GROUP * part for part in range(6)]
    take_low = edge_index(LOW[0] + LOW[1], all_parts, 1)
    take_high = edge_index(HIGH[0] + HIGH[1], all_parts, 0)
    ride_low = [
        edge_index([RIDE_LOW + EDGE * part for part in range(3)], all_parts[3 * s : 3 * s + 3], 1)
        for s in range(2)
    ]
    ride_high = [
        edge_index([RIDE_HIGH + EDGE * part for part in range(3)], all_parts[3 * s : 3 * s + 3], 0)
        for s in range(2)
    ]

    def unride(regions, start):
        cases = []
        for bases in regions:
            for part, base in enumerate(bases):
                cases.append((within(base, EDGE), lane - base + start + EDGE * part))
        return choose(cases, jnp.zeros_like(lane))

    leave_low = unride(LOW, RIDE_LOW)
    leave_high = unride(HIGH, RIDE_HIGH)

    def inside(bases, size):
        result = within(bases[0], size)
        for base in bases[1:]:
            result = jnp.logical_or(result, within(base, size))
        return result

    is_own = [within(OWN[s], 3 * GROUP) for s in range(2)]
    is_low = [inside(LOW[s], EDGE) for s in range(2)]

    reached = place_x + shift_x
    turn_x = []
    for part in range(6):
        s, c = part // 3, part % 3
        low = LOW[s][c] + 3 * place_y + reached + SIDE - 1
        high = HIGH[s][c] + 3 * place_y + jnp.minimum(reached - SIDE, 2)
        own = OWN[s] + GROUP * c + SIDE * place_y + reached
        turn_x.append(jnp.where(reached < 0, low, jnp.where(reached < SIDE, own, high)))

    def packed(parts):
        value = parts[0]
        for index in range(1, len(parts)):
            value = jnp.where(group == index, parts[index], value)
        return value

    def rows_of(line):
        return gather(jnp.broadcast_to(line, (8, 128)), unpack)

    MIDDLE = 0
    SENT = {0: 0, 1: deep + 1, -1: deep + 2 + tiles}
    HALO = {0: deep, 1: deep + 1 + tiles, -1: deep + 2 + 2 * tiles}

    def put(phase, blocks):
        last = deep - 1
        for k in range(deep):
            send[phase, MIDDLE + k] = blocks[k]
        send[phase, HALO[0]] = jnp.where(row < 4, blocks[0], blocks[last])
        for direction, take, ride, ride_at in (
            (1, take_low, ride_low, RIDE_LOW),
            (-1, take_high, ride_high, RIDE_HIGH),
        ):
            cut = {k: gather(blocks[k], take) for k in range(deep) if k not in riders or k == last}
            send[phase, HALO[direction]] = jnp.where(row < 4, cut[0], cut[last])
            for rider in riders:
                for s in range(2):
                    host = rider - 2 + s
                    cut[host] = jnp.where(
                        within(ride_at, 3 * EDGE), gather(blocks[rider], ride[s]), cut[host]
                    )
            for k in tile_of:
                send[phase, SENT[direction] + tile_of[k]] = cut[k]

    def exchange(phase):
        def start(src, dst, target):
            pltpu.make_async_remote_copy(
                src_ref=send.at[phase, src],
                dst_ref=held.at[phase, dst],
                send_sem=send_sems.at[phase],
                recv_sem=recv_sems.at[phase],
                device_id=target,
                device_id_type=MESH,
            ).start()

        for cx, cy in sorted(COLUMNS, key=lambda column: -abs(column[0]) - abs(column[1])):
            there = (-cx, -cy)
            if (cx, cy) != (0, 0):
                amount = tiles if cx else deep
                start(
                    pl.ds(SENT[cx], amount), pl.ds(slots[there], amount), neighbour(cx, cy, 0)
                )
            for ring in range(rings):
                start(
                    pl.ds(HALO[cx], 1),
                    pl.ds(halos[there] + ring, 1),
                    neighbour(cx, cy, -1 if ring == 0 else 1),
                )

    def wait_all(phase, sems):
        pltpu.make_async_copy(held.at[phase], held.at[phase], sems.at[phase]).wait()

    def merged_tiles(phase):
        result = {}
        for cy in (-1, 0, 1):
            def halo(cx):
                at = halos[cx, cy]
                if rings == 1:
                    return held[phase, at]
                return jnp.where(row < 4, held[phase, at], held[phase, at + 1])

            both = []
            for s in range(2):
                row_of_tiles = []
                for v in range(deep + 1):
                    k = v - 1
                    if v == 0:
                        low, own, high = halo(-1), halo(0), halo(1)
                    else:
                        own = send[phase, MIDDLE + k] if cy == 0 else held[phase, slots[0, cy] + k]
                        if k in riders:
                            host = tile_of[k - 2 + s]
                            low = gather(held[phase, slots[-1, cy] + host], leave_low)
                            high = gather(held[phase, slots[1, cy] + host], leave_high)
                        else:
                            low = held[phase, slots[-1, cy] + tile_of[k]]
                            high = held[phase, slots[1, cy] + tile_of[k]]
                    row_of_tiles.append(
                        jnp.where(is_own[s], own, jnp.where(is_low[s], low, high))
                    )
                both.append(row_of_tiles)
            result[cy] = both
        return result

    def by_shift_y(values, sy):
        if sy > 0:
            return jnp.where(place_y < sy, values[1], values[0])
        if sy < 0:
            return jnp.where(place_y >= SIDE + sy, values[-1], values[0])
        return values[0]

    def spread_out(tiles_in, out, parts):
        for v in range(deep + 1):
            for part in range(parts):
                lined = {
                    cy: gather(tiles_in[cy][part // 3][v], turn_x[part]) for cy in (-1, 0, 1)
                }
                for sy in SHIFTS:
                    value = by_shift_y(lined, sy)
                    out[sy + REACH, part, pl.ds(8 * v, 8), :] = value
                    if v == 0:
                        out[sy + REACH, part, pl.ds(8 * (deep + 1), 8), :] = value

    def contract(sums, parts, vec):
        xx, yy, zz, xy, xz, yz = parts
        for first in (0, 3):
            vx, vy, vz = vec[first : first + 3]
            sums[first] = sums[first] + (xx * vx + xy * vy + xz * vz)
            sums[first + 1] = sums[first + 1] + (xy * vx + yy * vy + yz * vz)
            sums[first + 2] = sums[first + 2] + (xz * vx + yz * vy + zz * vz)

    def tile_number(k, sy, sz):
        return (k * SPAN + sy + REACH) * SPAN + sz + REACH

    def build_tile(k, sy, sz):
        turn = sy % SIDE
        start = 8 + sz
        span = pl.ds(8 * k + start, 8)
        dx = near_geo[sy + REACH, 0, span, :] - own_ref[turn, k, 0]
        dy = near_geo[sy + REACH, 1, span, :] - (own_ref[turn, k, 1] - spacing * sy)
        dz = near_geo[sy + REACH, 2, span, :] - (own_ref[turn, k, 2] - spacing * sz)
        weight = switch[k, sy + REACH, pl.ds(start, 8), :]
        if sy == 0 and sz == 0:
            weight = jnp.where(group == REACH, 0.0, weight)
        square = jnp.maximum(dx * dx + dy * dy + dz * dz, 1.0)
        inverse = lax.rsqrt(square)
        inverse_square = inverse * inverse
        damp = square * square * inverse * (near_geo[sy + REACH, 3, span, :] * own_ref[turn, k, 3])
        damping = jnp.exp(-damp)
        fade = jnp.maximum(1.0 - square * (1.0 / cutoff_square), 0.0)
        scale = fade * fade * (inverse_square * inverse) * weight
        three = scale * (1.0 - damping)
        five = (1.0 - (1.0 + damp) * damping) * scale * (3.0 * inverse_square)
        tx, ty, tz = five * dx, five * dy, five * dz
        parts = (tx * dx - three, ty * dy - three, tz * dz - three, tx * dy, tx * dz, ty * dz)
        for part in range(6):
            tensor[tile_number(k, sy, sz), part] = parts[part]
        return parts

    def load_tile(k, sy, sz):
        return [tensor[tile_number(k, sy, sz), part] for part in range(6)]

    def fold(parts):
        width = GROUP
        while len(parts) > 1 or width < 128:
            upper = (lane // width) % 2 == 1
            merged = []
            for index in range(0, len(parts), 2):
                first = parts[index]
                second = parts[index + 1] if index + 1 < len(parts) else first
                kept = jnp.where(upper, second, first)
                moved = jnp.where(upper, first, second)
                merged.append(kept + pltpu.roll(moved, width, 1))
            parts = merged
            width *= 2
        return parts[0]

    def operate(make_tile, vector):
        image = []
        for k in range(deep):
            total = [None] * 6
            for turn in (1, 2, 3, 0):
                sums = [jnp.zeros((8, 128), jnp.float32)] * 6
                for sy in SHIFTS:
                    if sy % SIDE != turn:
                        continue
                    for sz in SHIFTS:
                        if abs(sy) == REACH and abs(sz) == REACH:
                            continue
                        span = pl.ds(8 * k + 8 + sz, 8)
                        vec = [near[sy + REACH, part, span, :] for part in range(6)]
                        contract(sums, make_tile(k, sy, sz), vec)
                for part in range(6):
                    value = sums[part]
                    if turn:
                        value = pltpu.roll(value, 128 - SIDE * turn, 1)
                    total[part] = value if total[part] is None else total[part] + value
            image.append(vector[k] / polar[k] - mask[k] * fold(total))
        return image

    def build_switch(tiles_in):
        def full(at):
            return jnp.full((8, 128), at, jnp.int32)

        def pick(first, second, third):
            return jnp.where(reached < 0, first, jnp.where(reached < SIDE, second, third))

        own_lane = OWN[1] + GROUP * (FLAGS - 3)
        for cz in (-1, 0, 1):
            active = [{} for _ in range(deep)]
            for cy in (-1, 0, 1):
                low, middle, high = (9 * (cx + 1) + 3 * (cy + 1) + cz + 1 for cx in (-1, 0, 1))
                low_at = full(LOW[1][FLAGS - 3] + 12 - low - 4)
                high_at = full(own_lane + flag_slot(high - 14))
                if middle < 13:
                    theirs = jnp.where(
                        reached < 0, low_at, full(own_lane + flag_slot(12 - middle))
                    )
                    ours = high_at
                else:
                    theirs = low_at
                    ours = jnp.where(
                        reached < SIDE, full(own_lane + flag_slot(max(middle - 14, 0))), high_at
                    )
                for k in range(deep):
                    v = (k + 1 + cz) % (deep + 1)
                    there = gather(tiles_in[cy][1][v], theirs)
                    here = gather(tiles_in[0][1][k + 1], ours)
                    value = pick(there, there if middle < 13 else here, here)
                    if middle == 13:
                        value = pick(value, 1.0, value)
                    active[k][cy] = jnp.where(group < SPAN, value, 0.0)
            for k in range(deep):
                for sy in SHIFTS:
                    switch[k, sy + REACH, pl.ds(8 * (cz + 1), 8), :] = by_shift_y(active[k], sy)

    in_set = [group < 3, jnp.logical_and(group >= 3, group < 6)]

    def start_sums(number, products):
        values = []
        for first, second in products:
            value = first[0] * second[0]
            for k in range(1, deep):
                value = value + first[k] * second[k]
            line = jnp.sum(value, axis=0, keepdims=True)
            for s in range(2):
                chosen = jnp.where(in_set[s][0:1], line, 0.0)
                values.append(jnp.sum(chosen, axis=1, keepdims=True))
        line = jnp.broadcast_to(values[0], (1, 128))
        for index in range(1, len(values)):
            line = jnp.where(group[0:1] == index, values[index], line)
        sums_out[number] = line
        sums_in[number, my_id] = line
        for step in range(1, total_devices):
            other = lax.rem(my_id + step, total_devices)
            pltpu.make_async_remote_copy(
                src_ref=sums_out.at[number],
                dst_ref=sums_in.at[number, my_id],
                send_sem=sum_send.at[number],
                recv_sem=sum_recv.at[number],
                device_id=device_at(other),
                device_id_type=MESH,
            ).start()

    def wait_sums(number, sems):
        rows = sums_in.at[number, pl.ds(0, total_devices - 1)]
        pltpu.make_async_copy(rows, rows, sems.at[number]).wait()

    def end_sums(number, amount):
        wait_sums(number, sum_recv)
        lines = [sums_in[number, index] for index in range(total_devices)]
        while len(lines) > 1:
            lines = [
                lines[index] + lines[index + 1] if index + 1 < len(lines) else lines[index]
                for index in range(0, len(lines), 2)
            ]
        line = jnp.broadcast_to(lines[0], (8, 128))
        return [
            gather(line, jnp.where(group < 3, GROUP * 2 * index, GROUP * (2 * index + 1)))
            for index in range(amount)
        ]

    def each(function, *vectors):
        return [function(k, *(vector[k] for vector in vectors)) for k in range(deep)]

    with scope("setup"):
        for copy in loads:
            copy.wait()
        site_x = spacing * (place_x.astype(jnp.float32) + 0.5)
        site_y = spacing * (place_y.astype(jnp.float32) + 0.5)
        site_z = spacing * (row.astype(jnp.float32) + 0.5)
        polar, mask, source, geometry = [], [], [], []
        for k in range(deep):
            places = [
                rows_of(coords_ref[3 * k + part]) - offset
                for part, offset in enumerate((site_x, site_y, site_z))
            ]
            polar_k = rows_of(polar_ref[k])
            mask_k = jnp.where(unpack < count_ref[k], 1.0, 0.0)
            root = lax.rsqrt(polar_k)
            slot = 14 + jnp.where(
                place_x == 0, place_y, 4 + 3 * place_y + place_x - 1
            )
            flag = pairs_ref[k, 0, 0] == slot
            for entry in range(1, 13):
                flag = jnp.logical_or(flag, pairs_ref[k, 0, entry] == slot)
            flags = jnp.where(flag, 1.0, 0.0)
            geometry.append(packed(places + [root, flags]))
            for turn in range(SIDE):
                for part, value in enumerate(places + [thole * root]):
                    if turn:
                        value = pltpu.roll(value, SIDE * turn, 1)
                    own_ref[turn, k, part] = value - far_x if part == 0 else value
            polar.append(polar_k)
            mask.append(mask_k)
            field_k = packed([rows_of(field_ref[6 * k + part]) for part in range(6)])
            source.append(field_k * mask_k)
        dipoles = each(lambda k, s: polar[k] * s, source)
        put(0, geometry)
        put(1, each(lambda k, d: d * mask[k], dipoles))
    with scope("barrier"):
        pl.semaphore_wait(barrier, total_devices - 1)
    with scope("send0"):
        exchange(0)
        exchange(1)
    with scope("geowait"):
        wait_all(0, recv_sems)
    with scope("geospread"):
        tiles_in = merged_tiles(0)
        spread_out(tiles_in, near_geo, 4)
        build_switch(tiles_in)
    with scope("wait0"):
        wait_all(1, recv_sems)
    with scope("build"):
        spread_out(merged_tiles(1), near, 6)
        image = operate(build_tile, dipoles)
    with scope("finish0"):
        residual = each(lambda k, s, a: s - a, source, image)
        precond = each(lambda k, r: polar[k] * r, residual)
        put(2, each(lambda k, p: p * mask[k], precond))
    with scope("send1"):
        exchange(2)
    with scope("wait1"):
        wait_all(2, recv_sems)
    with scope("apply1"):
        spread_out(merged_tiles(2), near, 6)
        image = operate(load_tile, precond)
    with scope("finish1"):
        turned = each(lambda k, q: polar[k] * q, image)
        put(3, each(lambda k, t: t * mask[k], turned))
    with scope("send2"):
        exchange(3)
    with scope("sum1"):
        start_sums(0, [(residual, precond), (precond, image)])
    with scope("wait2"):
        wait_all(3, recv_sems)
    with scope("apply2"):
        spread_out(merged_tiles(3), near, 6)
        turned_image = operate(load_tile, turned)
    with scope("sum1wait"):
        norm, curve = end_sums(0, 2)
    with scope("mid"):
        gamma = norm / curve
        dipoles = each(lambda k, d, p: d + gamma * p, dipoles, precond)
        residual = each(lambda k, r, q: r - gamma * q, residual, image)
        second = each(lambda k, r: polar[k] * r, residual)
        second_image = each(lambda k, q, t: q - gamma * t, image, turned_image)
        start_sums(
            1,
            [
                (residual, second), (second, second_image), (second, image),
                (precond, second_image),
            ],
        )
    with scope("sum2wait"):
        norm_next, second_curve, cross, cross_back = end_sums(1, 4)
    with scope("out"):
        ratio = norm_next / norm
        gamma = norm_next / (second_curve + ratio * (cross + cross_back + ratio * curve))
        for k in range(deep):
            direction = second[k] + ratio * precond[k]
            along = second_image[k] + ratio * image[k]
            for out, value in (
                (dip_out, dipoles[k] + gamma * direction),
                (res_out, residual[k] - gamma * along),
            ):
                for part in range(6):
                    turned_part = gather(value, GROUP * part + site)
                    line = jnp.where(group == row, turned_part, 0.0)
                    out[6 * k + part] = jnp.sum(line, axis=0, keepdims=True)
    with scope("sendwait"):
        for phase in range(4):
            wait_all(phase, send_sems)
        for number in range(2):
            wait_sums(number, sum_send)


def on_device(sizes, coords, polar, field, atom_count, pair_list):
    deep, slots = coords.shape[2], coords.shape[-1]
    assert coords.shape[0:2] == (1, 1) and slots == 128
    vmem = pl.BlockSpec(memory_space=pltpu.VMEM)
    hbm = pl.BlockSpec(memory_space=pl.ANY)
    rows = 8 * deep
    devices = sizes[0] * sizes[1] * sizes[2]
    tiles, total_tiles = (plan(deep, 1 if sizes[2] == 2 else 2)[index] for index in (2, 5))

    def buffer(*shape):
        return pltpu.VMEM(shape, jnp.float32)

    line = jax.ShapeDtypeStruct((6 * deep, 1, slots), jnp.float32)
    dma = pltpu.SemaphoreType.DMA
    dipoles, residual = pl.pallas_call(
        functools.partial(kernel, sizes, deep),
        out_shape=(line, line),
        in_specs=[hbm] * 5,
        out_specs=(vmem, vmem),
        scratch_shapes=[
            pltpu.SMEM((deep, 1, pair_list.shape[-1]), jnp.int32),
            pltpu.SMEM((deep,), jnp.int32),
            buffer(3 * deep, 1, slots),
            buffer(deep, 1, slots),
            buffer(6 * deep, 1, slots),
            buffer(4, deep + 2 * tiles + 3, 8, slots),
            buffer(4, total_tiles, 8, slots),
            buffer(SPAN, 6, rows + 16, slots),
            buffer(SPAN, 4, rows + 16, slots),
            buffer(SIDE, deep, 4, 8, slots),
            buffer(deep, SPAN, 24, slots),
            buffer(SPAN * SPAN * deep, 6, 8, slots),
            buffer(2, 1, slots),
            buffer(2, devices, 1, slots),
            dma((5,)),
            dma((4,)),
            dma((4,)),
            dma((2,)),
            dma((2,)),
        ],
        compiler_params=pltpu.CompilerParams(collective_id=0, has_side_effects=True),
    )(
        pair_list.reshape(deep, 1, -1),
        atom_count.reshape(deep),
        coords.reshape(3 * deep, 1, slots),
        polar.reshape(deep, 1, slots),
        field.reshape(6 * deep, 1, slots),
    )
    return dipoles.reshape(field.shape), residual.reshape(field.shape)


def solution(mesh):
    sizes = tuple(mesh.shape[name] for name in AXES)
    block = P(*AXES, None, None)
    return jax.shard_map(
        functools.partial(on_device, sizes),
        mesh=mesh,
        in_specs=(block, P(*AXES, None), block, P(*AXES), P(*AXES, None)),
        out_specs=(block, block),
        check_vma=False,
    )
```

time: 183 us -> 35.9 us (0.20)
  blocking collectives: 85.6 us -> 0 us
  starting transfers between devices: 24.8 us -> 0 us
  waiting for transfers between devices: 20.2 us -> 0 us
  Pallas kernels: 40.8 us -> 33.1 us
  other arithmetic: 6.43 us -> 0 us
  local copies, waits for them, and re-layouts: 5.45 us -> 1.91 us
    psum x2 -> x0, blocking collectives: 85.6 us -> none  [global_pair(): both = lax.psum(both, ('gx', 'gy', 'gz'))]
    ppermute x18 -> x0, starting transfers between devices: 24.8 us -> none  [the longest x9 14.6 us: extended(): lax.ppermute(head, axis, [((i + 1) % count, i) for i in range(count)])]
    ppermute x18 -> x0, waiting for transfers between devices: 20.2 us -> none  [the longest x9 16.6 us: extended(): lax.ppermute(tail, axis, [(i, (i + 1) % count) for i in range(count)])]
    pallas_call x3 -> x1, Pallas kernels: 40.8 us -> 33.1 us  [on_device(): pl.pallas_call(functools.partial(kernel, sizes, deep), out_shape=(line, l...]
    reduce_sum x6 -> x0, other arithmetic: 2.18 us -> none  [set_sums(): return jnp.sum(product, axis=(0, 1, 2, 4, 5))]
  transfers between devices with their start and end apart: 18 -> 0, of which waited for: 15 -> 0; matrix products, arithmetic and copies ran while one was open for 0% -> 0% of each run, Pallas kernels for 0% -> 0%
where the time goes in v2:
time: 35.9 us; the launch traced here: 35.6 us
  Pallas kernels  33.1 us (92%)
  local copies, waits for them, and re-layouts  1.91 us (5%)
  between operations  0.65 us (2%)
    pallas_call x1, Pallas kernels, on_device(): pl.pallas_call(functools.partial(kernel, sizes, deep), out_shape=(line, l...  33.1 us
    unnamed x4, local copies, waits for them, and re-layouts  1.91 us

profile of v2, /device:TPU:0, one launch (start us, length us, event | category | flops | bytes accessed | tf_op | source)
XLA Modules:
  0.0 35.6 jit_solution(11952237806610949889)
XLA Ops:
  0.6 33.1 %shard_map.68 = (f32[18,1,128]{2,1,0:T(1,128)}, f32[18,1,128]{2,1,0:T(1,128)}) custom-call(s32[3,1,13]{2,1,0:T(1,128)} %bitcast.15, s32[3]{0:T(128)} %bitcast.17, f32[9,1,128]{2,1,0:T(1,128)} %bitcast.14, f32[3,1,128]{2,1,0:T(1,128)} %bitcast.16, f32[18,1,128]{2,1,0:T(1,128)} %bitcast.11), custom_call_target="tpu_custom_call" | custom-call | tf_op jit(solution)/shard_map/pallas_call | solution.py:568
  33.7 0.0 copy-start
  33.7 1.3 %copy.11 = f32[1,1,3,6,128]{4,1,3,2,0:T(1,128)} copy(f32[1,1,3,6,128]{4,1,3,2,0:T(1,128)} %bitcast.13) | data formatting | bytes 18432
  35.0 0.0 copy-done
  35.0 0.6 %copy.12 = f32[1,1,3,6,128]{4,1,3,2,0:T(1,128)} copy(f32[1,1,3,6,128]{4,1,3,2,0:T(1,128)S(1)} %bitcast.12) | data formatting | bytes 18432
Async XLA Ops:
  33.7 1.3 %copy-start = (f32[18,1,128]{2,1,0:T(1,128)S(1)}, f32[18,1,128]{2,1,0:T(1,128)}, u32[]{:S(2)}) copy-start(f32[18,1,128]{2,1,0:T(1,128)} %get-tuple-element.5) | copy-start | bytes 27652

commit v3 on v2

--- a/solution.py
+++ b/solution.py
@@ -81,9 +81,19 @@
 
     with scope("signal"):
         barrier = pltpu.get_barrier_semaphore()
-        for step in range(1, total_devices):
-            other = lax.rem(my_id + step, total_devices)
-            pl.semaphore_signal(barrier, inc=1, device_id=device_at(other), device_id_type=MESH)
+        if max(sizes) <= 5:
+            steps = [(1, -1, 0) if size > 2 else (1, 0) for size in sizes]
+            greeted = [
+                neighbour(cx, cy, cz)
+                for cx in steps[0] for cy in steps[1] for cz in steps[2]
+                if (cx, cy, cz) != (0, 0, 0)
+            ]
+        else:
+            greeted = [
+                device_at(lax.rem(my_id + step, total_devices)) for step in range(1, total_devices)
+            ]
+        for target in greeted:
+            pl.semaphore_signal(barrier, inc=1, device_id=target, device_id_type=MESH)
         loads = [
             pltpu.make_async_copy(src, dst, load_sems.at[index])
             for index, (src, dst) in enumerate(
@@ -475,7 +485,7 @@
         put(0, geometry)
         put(1, each(lambda k, d: d * mask[k], dipoles))
     with scope("barrier"):
-        pl.semaphore_wait(barrier, total_devices - 1)
+        pl.semaphore_wait(barrier, len(greeted))
     with scope("send0"):
         exchange(0)
         exchange(1)
@@ -551,6 +561,17 @@
             wait_sums(number, sum_send)
 
 
+def store(dipoles, residual, dip_out, res_out, sems):
+    copies = [
+        pltpu.make_async_copy(dipoles, dip_out, sems.at[0]),
+        pltpu.make_async_copy(residual, res_out, sems.at[1]),
+    ]
+    for copy in copies:
+        copy.start()
+    for copy in copies:
+        copy.wait()
+
+
 def on_device(sizes, coords, polar, field, atom_count, pair_list):
     deep, slots = coords.shape[2], coords.shape[-1]
     assert coords.shape[0:2] == (1, 1) and slots == 128
@@ -563,7 +584,8 @@
     def buffer(*shape):
         return pltpu.VMEM(shape, jnp.float32)
 
-    line = jax.ShapeDtypeStruct((6 * deep, 1, slots), jnp.float32)
+    line = pltpu.VMEM((6 * deep, 1, slots), jnp.float32)
+    result = jax.ShapeDtypeStruct((6 * deep, 1, slots), jnp.float32)
     dma = pltpu.SemaphoreType.DMA
     dipoles, residual = pl.pallas_call(
         functools.partial(kernel, sizes, deep),
@@ -599,6 +621,16 @@
         polar.reshape(deep, 1, slots),
         field.reshape(6 * deep, 1, slots),
     )
+    dipoles, residual = pl.pallas_call(
+        store,
+        out_shape=(result, result),
+        in_specs=[vmem, vmem],
+        out_specs=(hbm, hbm),
+        scratch_shapes=[dma((2,))],
+    )(
+        pltpu.with_memory_space_constraint(dipoles, pltpu.VMEM),
+        pltpu.with_memory_space_constraint(residual, pltpu.VMEM),
+    )
     return dipoles.reshape(field.shape), residual.reshape(field.shape)
 
 

time: 35.9 us -> 33.8 us (0.942)
  local copies, waits for them, and re-layouts: 1.91 us -> 0 us
    unnamed x4 -> x0, local copies, waits for them, and re-layouts: 1.91 us -> none
    pallas_call x1, Pallas kernels: 33.1 us -> 32.4 us  [on_device(): pl.pallas_call(functools.partial(kernel, sizes, deep), out_shape=(line, l...]
    pallas_call x0 -> x1, Pallas kernels: none -> 0.62 us  [on_device(): pl.pallas_call(store, out_shape=(result, result), in_specs=[vmem, vmem],...]
where the time goes in v3:
time: 33.8 us; the launch traced here: 33.7 us
  Pallas kernels  33 us (98%)
  between operations  0.64 us (2%)
    pallas_call x1, Pallas kernels, on_device(): pl.pallas_call(functools.partial(kernel, sizes, deep), out_shape=(line, l...  32.4 us

profile of v3, /device:TPU:0, one launch (start us, length us, event | category | flops | bytes accessed | tf_op | source)
XLA Modules:
  0.0 33.7 jit_solution(6125725934761460600)
XLA Ops:
  0.6 32.4 %shard_map.68 = (f32[18,1,128]{2,1,0:T(1,128)S(1)}, f32[18,1,128]{2,1,0:T(1,128)S(1)}) custom-call(s32[3,1,13]{2,1,0:T(1,128)} %bitcast.13, s32[3]{0:T(128)} %bitcast.15, f32[9,1,128]{2,1,0:T(1,128)} %bitcast.12, f32[3,1,128]{2,1,0:T(1,128)} %bitcast.14, f32[18,1,128]{2,1,0:T(1,128)} %bitcast.11), custom_call_target="tpu_custom_call" | custom-call | tf_op jit(solution)/shard_map/pallas_call | solution.py:590
  33.0 0.6 %shard_map.69 = (f32[18,1,128]{2,1,0:T(1,128)}, f32[18,1,128]{2,1,0:T(1,128)}) custom-call(f32[18,1,128]{2,1,0:T(1,128)S(1)} %get-tuple-element.6.dipoles, f32[18,1,128]{2,1,0:T(1,128)S(1)} %get-tuple-element.7.residual), custom_call_target="tpu_custom_call" | custom-call | tf_op jit(solution)/shard_map/pallas_call | solution.py:624

commit v4 on v3

--- a/solution.py
+++ b/solution.py
@@ -16,6 +16,7 @@
 GROUP = SIDE * SIDE
 REACH = 3
 SHIFTS = range(-REACH, REACH + 1)
+PAGES = 1 + 2 * REACH
 SPAN = 2 * REACH + 1
 COLUMNS = [(cx, cy) for cx in (-1, 0, 1) for cy in (-1, 0, 1)]
 EDGE = 12
@@ -31,10 +32,6 @@
     return jnp.take_along_axis(value, index, axis=1, mode="promise_in_bounds")
 
 
-def flag_slot(flag):
-    return 4 * flag if flag < 4 else 4 * ((flag - 4) // 3) + 1 + (flag - 4) % 3
-
-
 def plan(deep, rings):
     riders = [k for k in range(deep) if k % 3 == 2]
     tile_of, tiles = {}, 0
@@ -42,16 +39,18 @@
         if k not in riders:
             tile_of[k] = tiles
             tiles += 1
-    slots, total = {}, 0
-    for column in COLUMNS:
-        if column != (0, 0):
-            slots[column] = total
-            total += tiles if column[0] else deep
-    halos = {}
-    for column in COLUMNS:
-        halos[column] = total
-        total += rings
-    return riders, tile_of, tiles, slots, halos, total
+    inner, halos, counts = {}, {}, {}
+    for cy in (0, 1):
+        total = 0
+        for cx in (-1, 0, 1):
+            if (cx, cy) != (0, 0):
+                inner[cx, cy] = total
+                total += tiles if cx else deep
+        for cx in (-1, 0, 1):
+            halos[cx, cy] = total
+            total += rings
+        counts[cy] = total
+    return riders, tile_of, tiles, inner, halos, counts
 
 
 def kernel(
@@ -61,10 +60,13 @@
 ):
     total_devices = sizes[0] * sizes[1] * sizes[2]
     rings = 1 if sizes[2] == 2 else 2
-    riders, tile_of, tiles, slots, halos, total_tiles = plan(deep, rings)
+    riders, tile_of, tiles, inner, halos, counts = plan(deep, rings)
     me = [lax.axis_index(name) for name in AXES]
     my_id = (me[0] * sizes[1] + me[1]) * sizes[2] + me[2]
     scope = jax.named_scope
+    up = jnp.where(2 * me[1] < sizes[1], 1, 0)
+    side_is_up = (None, up, 1 - up)
+    side_sign = (None, 2 * up - 1, 1 - 2 * up)
 
     def device_at(linear):
         return (
@@ -208,84 +210,95 @@
             for k in tile_of:
                 send[phase, SENT[direction] + tile_of[k]] = cut[k]
 
-    def exchange(phase):
-        def start(src, dst, target):
+    def place_of(cy):
+        return 0 if cy == 0 else counts[0] + counts[1] * (cy == 1)
+
+    def exchange(*phases):
+        def start(phase, src, at, there_y, amount, target):
             pltpu.make_async_remote_copy(
-                src_ref=send.at[phase, src],
-                dst_ref=held.at[phase, dst],
+                src_ref=send.at[phase, pl.ds(src, amount)],
+                dst_ref=held.at[phase, pl.ds(place_of(there_y) + at, amount)],
                 send_sem=send_sems.at[phase],
-                recv_sem=recv_sems.at[phase],
+                recv_sem=recv_sems.at[phase, 1 + there_y],
                 device_id=target,
                 device_id_type=MESH,
             ).start()
 
         for cx, cy in sorted(COLUMNS, key=lambda column: -abs(column[0]) - abs(column[1])):
-            there = (-cx, -cy)
-            if (cx, cy) != (0, 0):
-                amount = tiles if cx else deep
-                start(
-                    pl.ds(SENT[cx], amount), pl.ds(slots[there], amount), neighbour(cx, cy, 0)
-                )
-            for ring in range(rings):
-                start(
-                    pl.ds(HALO[cx], 1),
-                    pl.ds(halos[there] + ring, 1),
-                    neighbour(cx, cy, -1 if ring == 0 else 1),
-                )
+            for phase in phases:
+                if (cx, cy) != (0, 0):
+                    amount = tiles if cx else deep
+                    at = inner[-cx, abs(cy)]
+                    start(phase, SENT[cx], at, -cy, amount, neighbour(cx, cy, 0))
+                for ring in range(rings):
+                    at = halos[-cx, abs(cy)] + ring
+                    start(phase, HALO[cx], at, -cy, 1, neighbour(cx, cy, -1 if ring == 0 else 1))
+
+    def first_tile(stage):
+        return counts[0] + counts[1] * side_is_up[stage] if stage else 0
+
+    def arrival(phase, stage):
+        rows = held.at[phase, pl.ds(first_tile(stage), counts[1 if stage else 0])]
+        which = 1 + side_sign[stage] if stage else 1
+        pltpu.make_async_copy(rows, rows, recv_sems.at[phase, which]).wait()
 
     def wait_all(phase, sems):
         pltpu.make_async_copy(held.at[phase], held.at[phase], sems.at[phase]).wait()
 
-    def merged_tiles(phase):
-        result = {}
-        for cy in (-1, 0, 1):
-            def halo(cx):
-                at = halos[cx, cy]
-                if rings == 1:
-                    return held[phase, at]
-                return jnp.where(row < 4, held[phase, at], held[phase, at + 1])
-
-            both = []
-            for s in range(2):
-                row_of_tiles = []
-                for v in range(deep + 1):
-                    k = v - 1
-                    if v == 0:
-                        low, own, high = halo(-1), halo(0), halo(1)
+    def merged_tiles(phase, stage):
+        first = first_tile(stage)
+        far = 1 if stage else 0
+
+        def halo(cx):
+            at = first + halos[cx, far]
+            if rings == 1:
+                return held[phase, at]
+            return jnp.where(row < 4, held[phase, at], held[phase, at + 1])
+
+        def tile(cx, number):
+            return held[phase, first + inner[cx, far] + number]
+
+        both = []
+        for s in range(2):
+            row_of_tiles = []
+            for v in range(deep + 1):
+                k = v - 1
+                if v == 0:
+                    low, own, high = halo(-1), halo(0), halo(1)
+                else:
+                    own = tile(0, k) if stage else send[phase, MIDDLE + k]
+                    if k in riders:
+                        host = tile_of[k - 2 + s]
+                        low = gather(tile(-1, host), leave_low)
+                        high = gather(tile(1, host), leave_high)
                     else:
-                        own = send[phase, MIDDLE + k] if cy == 0 else held[phase, slots[0, cy] + k]
-                        if k in riders:
-                            host = tile_of[k - 2 + s]
-                            low = gather(held[phase, slots[-1, cy] + host], leave_low)
-                            high = gather(held[phase, slots[1, cy] + host], leave_high)
-                        else:
-                            low = held[phase, slots[-1, cy] + tile_of[k]]
-                            high = held[phase, slots[1, cy] + tile_of[k]]
-                    row_of_tiles.append(
-                        jnp.where(is_own[s], own, jnp.where(is_low[s], low, high))
-                    )
-                both.append(row_of_tiles)
-            result[cy] = both
-        return result
-
-    def by_shift_y(values, sy):
-        if sy > 0:
-            return jnp.where(place_y < sy, values[1], values[0])
-        if sy < 0:
-            return jnp.where(place_y >= SIDE + sy, values[-1], values[0])
-        return values[0]
-
-    def spread_out(tiles_in, out, parts):
+                        low, high = tile(-1, tile_of[k]), tile(1, tile_of[k])
+                row_of_tiles.append(jnp.where(is_own[s], own, jnp.where(is_low[s], low, high)))
+            both.append(row_of_tiles)
+        return both
+
+    def page_of(stage, j):
+        return REACH * (stage - 1) + j if stage else 0
+
+    depth_y = [None] + [
+        jnp.where(side_is_up[stage] > 0, place_y, SIDE - 1 - place_y) for stage in (1, 2)
+    ]
+
+    def spread_out(tiles_in, out, parts, stage):
         for v in range(deep + 1):
             for part in range(parts):
-                lined = {
-                    cy: gather(tiles_in[cy][part // 3][v], turn_x[part]) for cy in (-1, 0, 1)
-                }
-                for sy in SHIFTS:
-                    value = by_shift_y(lined, sy)
-                    out[sy + REACH, part, pl.ds(8 * v, 8), :] = value
+                value = gather(tiles_in[part // 3][v], turn_x[part])
+                pages = {0: value}
+                if stage:
+                    base = out[0, part, pl.ds(8 * v, 8), :]
+                    pages = {
+                        page_of(stage, j): jnp.where(depth_y[stage] < j, value, base)
+                        for j in range(1, REACH + 1)
+                    }
+                for page, value in pages.items():
+                    out[page, part, pl.ds(8 * v, 8), :] = value
                     if v == 0:
-                        out[sy + REACH, part, pl.ds(8 * (deep + 1), 8), :] = value
+                        out[page, part, pl.ds(8 * (deep + 1), 8), :] = value
 
     def contract(sums, parts, vec):
         xx, yy, zz, xy, xz, yz = parts
@@ -295,23 +308,22 @@
             sums[first + 1] = sums[first + 1] + (xy * vx + yy * vy + yz * vz)
             sums[first + 2] = sums[first + 2] + (xz * vx + yz * vy + zz * vz)
 
-    def tile_number(k, sy, sz):
-        return (k * SPAN + sy + REACH) * SPAN + sz + REACH
-
-    def build_tile(k, sy, sz):
-        turn = sy % SIDE
+    def tile_number(k, page, sz):
+        return (k * PAGES + page) * SPAN + sz + REACH
+
+    def build_tile(k, page, sz):
         start = 8 + sz
         span = pl.ds(8 * k + start, 8)
-        dx = near_geo[sy + REACH, 0, span, :] - own_ref[turn, k, 0]
-        dy = near_geo[sy + REACH, 1, span, :] - (own_ref[turn, k, 1] - spacing * sy)
-        dz = near_geo[sy + REACH, 2, span, :] - (own_ref[turn, k, 2] - spacing * sz)
-        weight = switch[k, sy + REACH, pl.ds(start, 8), :]
-        if sy == 0 and sz == 0:
+        dx = near_geo[page, 0, span, :] - own_ref[page, k, 0]
+        dy = near_geo[page, 1, span, :] - own_ref[page, k, 1]
+        dz = near_geo[page, 2, span, :] - (own_ref[page, k, 2] - spacing * sz)
+        weight = switch[k, page, pl.ds(start, 8), :]
+        if page == 0 and sz == 0:
             weight = jnp.where(group == REACH, 0.0, weight)
         square = jnp.maximum(dx * dx + dy * dy + dz * dz, 1.0)
         inverse = lax.rsqrt(square)
         inverse_square = inverse * inverse
-        damp = square * square * inverse * (near_geo[sy + REACH, 3, span, :] * own_ref[turn, k, 3])
+        damp = square * square * inverse * (near_geo[page, 3, span, :] * own_ref[page, k, 3])
         damping = jnp.exp(-damp)
         fade = jnp.maximum(1.0 - square * (1.0 / cutoff_square), 0.0)
         scale = fade * fade * (inverse_square * inverse) * weight
@@ -320,11 +332,11 @@
         tx, ty, tz = five * dx, five * dy, five * dz
         parts = (tx * dx - three, ty * dy - three, tz * dz - three, tx * dy, tx * dz, ty * dz)
         for part in range(6):
-            tensor[tile_number(k, sy, sz), part] = parts[part]
+            tensor[tile_number(k, page, sz), part] = parts[part]
         return parts
 
-    def load_tile(k, sy, sz):
-        return [tensor[tile_number(k, sy, sz), part] for part in range(6)]
+    def load_tile(k, page, sz):
+        return [tensor[tile_number(k, page, sz), part] for part in range(6)]
 
     def fold(parts):
         width = GROUP
@@ -341,64 +353,71 @@
             width *= 2
         return parts[0]
 
-    def operate(make_tile, vector):
+    def add_stage(make_tile, totals, stage, k):
+        for j in range(1, REACH + 1) if stage else [0]:
+            sums = [jnp.zeros((8, 128), jnp.float32)] * 6
+            page = page_of(stage, j)
+            for sz in SHIFTS:
+                if j == REACH and abs(sz) == REACH:
+                    continue
+                span = pl.ds(8 * k + 8 + sz, 8)
+                vec = [near[page, part, span, :] for part in range(6)]
+                contract(sums, make_tile(k, page, sz), vec)
+            for part in range(6):
+                if stage:
+                    back = 128 - SIDE * side_sign[stage] * j
+                    value = pltpu.roll(sums[part], lax.rem(back, 128), 1)
+                    totals[k][part] = totals[k][part] + value
+                else:
+                    totals[k][part] = sums[part]
+
+    def operate(phase, make_tile, vector, prepare=None):
+        totals = [[None] * 6 for _ in range(deep)]
         image = []
-        for k in range(deep):
-            total = [None] * 6
-            for turn in (1, 2, 3, 0):
-                sums = [jnp.zeros((8, 128), jnp.float32)] * 6
-                for sy in SHIFTS:
-                    if sy % SIDE != turn:
-                        continue
-                    for sz in SHIFTS:
-                        if abs(sy) == REACH and abs(sz) == REACH:
-                            continue
-                        span = pl.ds(8 * k + 8 + sz, 8)
-                        vec = [near[sy + REACH, part, span, :] for part in range(6)]
-                        contract(sums, make_tile(k, sy, sz), vec)
-                for part in range(6):
-                    value = sums[part]
-                    if turn:
-                        value = pltpu.roll(value, 128 - SIDE * turn, 1)
-                    total[part] = value if total[part] is None else total[part] + value
-            image.append(vector[k] / polar[k] - mask[k] * fold(total))
+        for stage in range(3):
+            if prepare is not None:
+                prepare(stage)
+            with scope(f"arrive{phase}_{stage}"):
+                arrival(phase, stage)
+            with scope(f"stage{phase}_{stage}"):
+                spread_out(merged_tiles(phase, stage), near, 6, stage)
+                for k in range(deep):
+                    add_stage(make_tile, totals, stage, k)
+                    if stage == 2:
+                        image.append(vector[k] / polar[k] - mask[k] * fold(totals[k]))
         return image
 
-    def build_switch(tiles_in):
+    def build_switch(tiles_in, stage):
         def full(at):
-            return jnp.full((8, 128), at, jnp.int32)
-
-        def pick(first, second, third):
-            return jnp.where(reached < 0, first, jnp.where(reached < SIDE, second, third))
+            return jnp.broadcast_to(jnp.asarray(at, jnp.int32), (8, 128))
 
         own_lane = OWN[1] + GROUP * (FLAGS - 3)
+        low_lane = LOW[1][FLAGS - 3]
+        cy = side_sign[stage] if stage else 0
         for cz in (-1, 0, 1):
-            active = [{} for _ in range(deep)]
-            for cy in (-1, 0, 1):
-                low, middle, high = (9 * (cx + 1) + 3 * (cy + 1) + cz + 1 for cx in (-1, 0, 1))
-                low_at = full(LOW[1][FLAGS - 3] + 12 - low - 4)
-                high_at = full(own_lane + flag_slot(high - 14))
-                if middle < 13:
-                    theirs = jnp.where(
-                        reached < 0, low_at, full(own_lane + flag_slot(12 - middle))
+            low_at = full(low_lane + 7 - 3 * (cy + 1) - cz)
+            high_at = full(own_lane + SIDE * (cy + 1) + cz + 2)
+            middle_at = full(own_lane + SIDE * (2 + cy * cz) if stage else own_lane)
+            theirs = jnp.where(reached < 0, low_at, middle_at)
+            ours = jnp.where(reached < SIDE, middle_at, high_at)
+            ahead = cy > 0 if stage else cz > 0
+            use_own = jnp.where(ahead, reached, reached - SIDE) >= 0
+            for k in range(deep):
+                v = (k + 1 + cz) % (deep + 1)
+                there = gather(tiles_in[1][v], theirs)
+                here = gather(send[0, MIDDLE + k], ours)
+                value = jnp.where(use_own, here, there)
+                if stage == 0 and cz == 0:
+                    inside_own = jnp.logical_and(reached >= 0, reached < SIDE)
+                    value = jnp.where(inside_own, 1.0, value)
+                value = jnp.where(group < SPAN, value, 0.0)
+                span = pl.ds(8 * (cz + 1), 8)
+                if stage == 0:
+                    switch[k, 0, span, :] = value
+                for j in range(1, REACH + 1) if stage else []:
+                    switch[k, page_of(stage, j), span, :] = jnp.where(
+                        depth_y[stage] < j, value, switch[k, 0, span, :]
                     )
-                    ours = high_at
-                else:
-                    theirs = low_at
-                    ours = jnp.where(
-                        reached < SIDE, full(own_lane + flag_slot(max(middle - 14, 0))), high_at
-                    )
-                for k in range(deep):
-                    v = (k + 1 + cz) % (deep + 1)
-                    there = gather(tiles_in[cy][1][v], theirs)
-                    here = gather(tiles_in[0][1][k + 1], ours)
-                    value = pick(there, there if middle < 13 else here, here)
-                    if middle == 13:
-                        value = pick(value, 1.0, value)
-                    active[k][cy] = jnp.where(group < SPAN, value, 0.0)
-            for k in range(deep):
-                for sy in SHIFTS:
-                    switch[k, sy + REACH, pl.ds(8 * (cz + 1), 8), :] = by_shift_y(active[k], sy)
 
     in_set = [group < 3, jnp.logical_and(group >= 3, group < 6)]
 
@@ -472,11 +491,15 @@
                 flag = jnp.logical_or(flag, pairs_ref[k, 0, entry] == slot)
             flags = jnp.where(flag, 1.0, 0.0)
             geometry.append(packed(places + [root, flags]))
-            for turn in range(SIDE):
-                for part, value in enumerate(places + [thole * root]):
-                    if turn:
-                        value = pltpu.roll(value, SIDE * turn, 1)
-                    own_ref[turn, k, part] = value - far_x if part == 0 else value
+            for stage in range(3):
+                for j in range(1, REACH + 1) if stage else [0]:
+                    for part, value in enumerate(places + [thole * root]):
+                        if stage:
+                            shift_y = side_sign[stage] * j
+                            value = pltpu.roll(value, lax.rem(128 + SIDE * shift_y, 128), 1)
+                            if part == 1:
+                                value = value - spacing * shift_y.astype(jnp.float32)
+                        own_ref[page_of(stage, j), k, part] = value - far_x if part == 0 else value
             polar.append(polar_k)
             mask.append(mask_k)
             field_k = packed([rows_of(field_ref[6 * k + part]) for part in range(6)])
@@ -487,30 +510,24 @@
     with scope("barrier"):
         pl.semaphore_wait(barrier, len(greeted))
     with scope("send0"):
-        exchange(0)
-        exchange(1)
-    with scope("geowait"):
-        wait_all(0, recv_sems)
-    with scope("geospread"):
-        tiles_in = merged_tiles(0)
-        spread_out(tiles_in, near_geo, 4)
-        build_switch(tiles_in)
-    with scope("wait0"):
-        wait_all(1, recv_sems)
-    with scope("build"):
-        spread_out(merged_tiles(1), near, 6)
-        image = operate(build_tile, dipoles)
+        exchange(0, 1)
+
+    def prepare(stage):
+        with scope(f"geoarrive_{stage}"):
+            arrival(0, stage)
+        with scope(f"geo_{stage}"):
+            tiles_in = merged_tiles(0, stage)
+            spread_out(tiles_in, near_geo, 4, stage)
+            build_switch(tiles_in, stage)
+
+    image = operate(1, build_tile, dipoles, prepare)
     with scope("finish0"):
         residual = each(lambda k, s, a: s - a, source, image)
         precond = each(lambda k, r: polar[k] * r, residual)
         put(2, each(lambda k, p: p * mask[k], precond))
     with scope("send1"):
         exchange(2)
-    with scope("wait1"):
-        wait_all(2, recv_sems)
-    with scope("apply1"):
-        spread_out(merged_tiles(2), near, 6)
-        image = operate(load_tile, precond)
+    image = operate(2, load_tile, precond)
     with scope("finish1"):
         turned = each(lambda k, q: polar[k] * q, image)
         put(3, each(lambda k, t: t * mask[k], turned))
@@ -518,11 +535,7 @@
         exchange(3)
     with scope("sum1"):
         start_sums(0, [(residual, precond), (precond, image)])
-    with scope("wait2"):
-        wait_all(3, recv_sems)
-    with scope("apply2"):
-        spread_out(merged_tiles(3), near, 6)
-        turned_image = operate(load_tile, turned)
+    turned_image = operate(3, load_tile, turned)
     with scope("sum1wait"):
         norm, curve = end_sums(0, 2)
     with scope("mid"):
@@ -579,7 +592,7 @@
     hbm = pl.BlockSpec(memory_space=pl.ANY)
     rows = 8 * deep
     devices = sizes[0] * sizes[1] * sizes[2]
-    tiles, total_tiles = (plan(deep, 1 if sizes[2] == 2 else 2)[index] for index in (2, 5))
+    tiles, counts = (plan(deep, 1 if sizes[2] == 2 else 2)[index] for index in (2, 5))
 
     def buffer(*shape):
         return pltpu.VMEM(shape, jnp.float32)
@@ -599,17 +612,17 @@
             buffer(deep, 1, slots),
             buffer(6 * deep, 1, slots),
             buffer(4, deep + 2 * tiles + 3, 8, slots),
-            buffer(4, total_tiles, 8, slots),
-            buffer(SPAN, 6, rows + 16, slots),
-            buffer(SPAN, 4, rows + 16, slots),
-            buffer(SIDE, deep, 4, 8, slots),
-            buffer(deep, SPAN, 24, slots),
-            buffer(SPAN * SPAN * deep, 6, 8, slots),
+            buffer(4, counts[0] + 2 * counts[1], 8, slots),
+            buffer(PAGES, 6, rows + 16, slots),
+            buffer(PAGES, 4, rows + 16, slots),
+            buffer(PAGES, deep, 4, 8, slots),
+            buffer(deep, PAGES, 24, slots),
+            buffer(PAGES * SPAN * deep, 6, 8, slots),
             buffer(2, 1, slots),
             buffer(2, devices, 1, slots),
             dma((5,)),
             dma((4,)),
-            dma((4,)),
+            dma((4, 3)),
             dma((2,)),
             dma((2,)),
         ],

time: 33.8 us -> 31.6 us (0.935)
  Pallas kernels: 33 us -> 30.8 us
    pallas_call x1, Pallas kernels: 32.4 us -> 30.2 us  [on_device(): pl.pallas_call(functools.partial(kernel, sizes, deep), out_shape=(line, l...]
where the time goes in v4:
time: 31.6 us; the launch traced here: 31.5 us
  Pallas kernels  30.8 us (97%)
  between operations  0.64 us (2%)
    pallas_call x1, Pallas kernels, on_device(): pl.pallas_call(functools.partial(kernel, sizes, deep), out_shape=(line, l...  30.2 us

profile of v4, /device:TPU:0, one launch (start us, length us, event | category | flops | bytes accessed | tf_op | source)
XLA Modules:
  0.0 31.5 jit_solution(1845086418724143842)
XLA Ops:
  0.6 30.2 %shard_map.68 = (f32[18,1,128]{2,1,0:T(1,128)S(1)}, f32[18,1,128]{2,1,0:T(1,128)S(1)}) custom-call(s32[3,1,13]{2,1,0:T(1,128)} %bitcast.13, s32[3]{0:T(128)} %bitcast.15, f32[9,1,128]{2,1,0:T(1,128)} %bitcast.12, f32[3,1,128]{2,1,0:T(1,128)} %bitcast.14, f32[18,1,128]{2,1,0:T(1,128)} %bitcast.11), custom_call_target="tpu_custom_call" | custom-call | tf_op jit(solution)/shard_map/pallas_call | solution.py:603
  30.9 0.6 %shard_map.69 = (f32[18,1,128]{2,1,0:T(1,128)}, f32[18,1,128]{2,1,0:T(1,128)}) custom-call(f32[18,1,128]{2,1,0:T(1,128)S(1)} %get-tuple-element.6.dipoles, f32[18,1,128]{2,1,0:T(1,128)S(1)} %get-tuple-element.7.residual), custom_call_target="tpu_custom_call" | custom-call | tf_op jit(solution)/shard_map/pallas_call | solution.py:637

commit v5 on v4

--- a/solution.py
+++ b/solution.py
@@ -18,6 +18,7 @@
 SHIFTS = range(-REACH, REACH + 1)
 PAGES = 1 + 2 * REACH
 SPAN = 2 * REACH + 1
+ORDER = [(2, -1), (2, 1), (1, -1), (1, 1), (2, 0), (0, -1), (0, 1), (1, 0), (0, 0)]
 COLUMNS = [(cx, cy) for cx in (-1, 0, 1) for cy in (-1, 0, 1)]
 EDGE = 12
 OWN = (0, 48)
@@ -55,8 +56,8 @@
 
 def kernel(
     sizes, deep, pairs_hbm, count_hbm, coords_hbm, polar_hbm, field_hbm, dip_out, res_out,
-    pairs_ref, count_ref, coords_ref, polar_ref, field_ref, send, held, near, near_geo, own_ref,
-    switch, tensor, sums_out, sums_in, load_sems, send_sems, recv_sems, sum_send, sum_recv,
+    pairs_ref, count_ref, lines, send, held, near, near_geo, own_ref,
+    switch, tensor, sums_out, sums_in, load_sem, send_sem, recv_sems, sum_send, sum_recv,
 ):
     total_devices = sizes[0] * sizes[1] * sizes[2]
     rings = 1 if sizes[2] == 2 else 2
@@ -96,20 +97,17 @@
             ]
         for target in greeted:
             pl.semaphore_signal(barrier, inc=1, device_id=target, device_id_type=MESH)
-        loads = [
-            pltpu.make_async_copy(src, dst, load_sems.at[index])
-            for index, (src, dst) in enumerate(
-                (
-                    (pairs_hbm, pairs_ref),
-                    (count_hbm, count_ref),
-                    (coords_hbm, coords_ref),
-                    (polar_hbm, polar_ref),
-                    (field_hbm, field_ref),
-                )
-            )
-        ]
-        for copy in loads:
-            copy.start()
+        coords_ref = lines.at[pl.ds(0, 3 * deep)]
+        polar_ref = lines.at[pl.ds(3 * deep, deep)]
+        field_ref = lines.at[pl.ds(4 * deep, 6 * deep)]
+        for src, dst, sem in (
+            (coords_hbm, coords_ref, load_sem),
+            (polar_hbm, polar_ref, load_sem),
+            (field_hbm, field_ref, load_sem),
+            (pairs_hbm, pairs_ref, send_sem),
+            (count_hbm, count_ref, sum_send),
+        ):
+            pltpu.make_async_copy(src, dst, sem).start()
 
     lane = lax.broadcasted_iota(jnp.int32, (8, 128), 1)
     row = lax.broadcasted_iota(jnp.int32, (8, 128), 0)
@@ -210,40 +208,41 @@
             for k in tile_of:
                 send[phase, SENT[direction] + tile_of[k]] = cut[k]
 
-    def place_of(cy):
-        return 0 if cy == 0 else counts[0] + counts[1] * (cy == 1)
-
     def exchange(*phases):
-        def start(phase, src, at, there_y, amount, target):
+        def start(phase, src, at, stage, amount, target):
+            place = counts[0] + counts[1] * (1 - side_is_up[stage]) if stage else 0
             pltpu.make_async_remote_copy(
                 src_ref=send.at[phase, pl.ds(src, amount)],
-                dst_ref=held.at[phase, pl.ds(place_of(there_y) + at, amount)],
-                send_sem=send_sems.at[phase],
-                recv_sem=recv_sems.at[phase, 1 + there_y],
+                dst_ref=held.at[phase, pl.ds(place + at, amount)],
+                send_sem=send_sem,
+                recv_sem=recv_sems.at[max(phase - 1, 0), 1 - side_sign[stage] if stage else 1],
                 device_id=target,
                 device_id_type=MESH,
             ).start()
 
-        for cx, cy in sorted(COLUMNS, key=lambda column: -abs(column[0]) - abs(column[1])):
+        for stage, cx in ORDER:
+            cy = side_sign[stage] if stage else 0
+            far = 1 if stage else 0
             for phase in phases:
-                if (cx, cy) != (0, 0):
+                if stage or cx:
                     amount = tiles if cx else deep
-                    at = inner[-cx, abs(cy)]
-                    start(phase, SENT[cx], at, -cy, amount, neighbour(cx, cy, 0))
+                    start(
+                        phase, SENT[cx], inner[-cx, far], stage, amount, neighbour(cx, cy, 0)
+                    )
                 for ring in range(rings):
-                    at = halos[-cx, abs(cy)] + ring
-                    start(phase, HALO[cx], at, -cy, 1, neighbour(cx, cy, -1 if ring == 0 else 1))
+                    at = halos[-cx, far] + ring
+                    target = neighbour(cx, cy, -1 if ring == 0 else 1)
+                    start(phase, HALO[cx], at, stage, 1, target)
 
     def first_tile(stage):
         return counts[0] + counts[1] * side_is_up[stage] if stage else 0
 
     def arrival(phase, stage):
-        rows = held.at[phase, pl.ds(first_tile(stage), counts[1 if stage else 0])]
+        number = max(phase - 1, 0)
+        first = pl.ds(0, 2) if number == 0 else pl.ds(phase, 1)
+        rows = held.at[first, pl.ds(first_tile(stage), counts[1 if stage else 0])]
         which = 1 + side_sign[stage] if stage else 1
-        pltpu.make_async_copy(rows, rows, recv_sems.at[phase, which]).wait()
-
-    def wait_all(phase, sems):
-        pltpu.make_async_copy(held.at[phase], held.at[phase], sems.at[phase]).wait()
+        pltpu.make_async_copy(rows, rows, recv_sems.at[number, which]).wait()
 
     def merged_tiles(phase, stage):
         first = first_tile(stage)
@@ -338,20 +337,34 @@
     def load_tile(k, page, sz):
         return [tensor[tile_number(k, page, sz), part] for part in range(6)]
 
-    def fold(parts):
-        width = GROUP
-        while len(parts) > 1 or width < 128:
-            upper = (lane // width) % 2 == 1
-            merged = []
-            for index in range(0, len(parts), 2):
-                first = parts[index]
-                second = parts[index + 1] if index + 1 < len(parts) else first
-                kept = jnp.where(upper, second, first)
-                moved = jnp.where(upper, first, second)
-                merged.append(kept + pltpu.roll(moved, width, 1))
-            parts = merged
-            width *= 2
-        return parts[0]
+    def back_roll(stage, j):
+        return lax.rem(128 - SIDE * side_sign[stage] * j, 128) if stage else 0
+
+    def gather_groups(sums, stage, j, total):
+        back = back_roll(stage, j)
+        ends_in = (lane + back) // GROUP % 8
+        first, second = total
+        for step in range(4):
+            comes = (ends_in + step) % 4
+            quad = sums[3]
+            for part in range(3):
+                quad = jnp.where(comes == part, sums[part], quad)
+            pair = jnp.where(comes % 2 == 0, sums[4], sums[5])
+            shift = back + GROUP * step
+            if stage:
+                shift = lax.rem(shift, 128)
+            if stage or step:
+                quad, pair = pltpu.roll(quad, shift, 1), pltpu.roll(pair, shift, 1)
+            first = quad if first is None else first + quad
+            second = pair if second is None else second + pair
+        return first, second
+
+    upper = group >= 4
+
+    def fold(total):
+        kept = jnp.where(upper, total[1], total[0])
+        moved = jnp.where(upper, total[0], total[1])
+        return kept + pltpu.roll(moved, 64, 1)
 
     def add_stage(make_tile, totals, stage, k):
         for j in range(1, REACH + 1) if stage else [0]:
@@ -363,22 +376,16 @@
                 span = pl.ds(8 * k + 8 + sz, 8)
                 vec = [near[page, part, span, :] for part in range(6)]
                 contract(sums, make_tile(k, page, sz), vec)
-            for part in range(6):
-                if stage:
-                    back = 128 - SIDE * side_sign[stage] * j
-                    value = pltpu.roll(sums[part], lax.rem(back, 128), 1)
-                    totals[k][part] = totals[k][part] + value
-                else:
-                    totals[k][part] = sums[part]
+            totals[k] = gather_groups(sums, stage, j, totals[k])
 
     def operate(phase, make_tile, vector, prepare=None):
-        totals = [[None] * 6 for _ in range(deep)]
+        totals = [(None, None)] * deep
         image = []
         for stage in range(3):
+            with scope(f"arrive{phase}_{stage}"):
+                arrival(phase, stage)
             if prepare is not None:
                 prepare(stage)
-            with scope(f"arrive{phase}_{stage}"):
-                arrival(phase, stage)
             with scope(f"stage{phase}_{stage}"):
                 spread_out(merged_tiles(phase, stage), near, 6, stage)
                 for k in range(deep):
@@ -419,6 +426,15 @@
                         depth_y[stage] < j, value, switch[k, 0, span, :]
                     )
 
+    everyone = []
+    for far in list(range(1, sizes[1])) + [0]:
+        y = lax.rem(me[1] + side_sign[2] * far + sizes[1], sizes[1])
+        for cx in range(sizes[0]):
+            x = lax.rem(me[0] + cx, sizes[0])
+            for cz in range(sizes[2]):
+                if far or cx or cz:
+                    everyone.append((x, y, lax.rem(me[2] + cz, sizes[2])))
+
     in_set = [group < 3, jnp.logical_and(group >= 3, group < 6)]
 
     def start_sums(number, products):
@@ -436,41 +452,44 @@
             line = jnp.where(group[0:1] == index, values[index], line)
         sums_out[number] = line
         sums_in[number, my_id] = line
-        for step in range(1, total_devices):
-            other = lax.rem(my_id + step, total_devices)
+        for target in everyone:
             pltpu.make_async_remote_copy(
                 src_ref=sums_out.at[number],
                 dst_ref=sums_in.at[number, my_id],
-                send_sem=sum_send.at[number],
+                send_sem=sum_send,
                 recv_sem=sum_recv.at[number],
-                device_id=device_at(other),
+                device_id=target,
                 device_id_type=MESH,
             ).start()
 
-    def wait_sums(number, sems):
+    def end_sums(number):
         rows = sums_in.at[number, pl.ds(0, total_devices - 1)]
-        pltpu.make_async_copy(rows, rows, sems.at[number]).wait()
-
-    def end_sums(number, amount):
-        wait_sums(number, sum_recv)
+        pltpu.make_async_copy(rows, rows, sum_recv.at[number]).wait()
         lines = [sums_in[number, index] for index in range(total_devices)]
         while len(lines) > 1:
             lines = [
                 lines[index] + lines[index + 1] if index + 1 < len(lines) else lines[index]
                 for index in range(0, len(lines), 2)
             ]
-        line = jnp.broadcast_to(lines[0], (8, 128))
-        return [
-            gather(line, jnp.where(group < 3, GROUP * 2 * index, GROUP * (2 * index + 1)))
-            for index in range(amount)
-        ]
+        return jnp.broadcast_to(lines[0], (8, 128))
+
+    def total_by(first_set, line, index):
+        return gather(line, jnp.where(first_set, GROUP * 2 * index, GROUP * (2 * index + 1)))
+
+    def as_rows(value):
+        result = value
+        for step in range(1, 8):
+            moved = pltpu.roll(pltpu.roll(value, 8 - step, 0), GROUP * step, 1)
+            result = jnp.where((group - row) % 8 == step, moved, result)
+        return result
 
     def each(function, *vectors):
         return [function(k, *(vector[k] for vector in vectors)) for k in range(deep)]
 
     with scope("setup"):
-        for copy in loads:
-            copy.wait()
+        pltpu.make_async_copy(lines, lines, load_sem).wait()
+        pltpu.make_async_copy(pairs_hbm, pairs_ref, send_sem).wait()
+        pltpu.make_async_copy(count_hbm, count_ref, sum_send).wait()
         site_x = spacing * (place_x.astype(jnp.float32) + 0.5)
         site_y = spacing * (place_y.astype(jnp.float32) + 0.5)
         site_z = spacing * (row.astype(jnp.float32) + 0.5)
@@ -513,8 +532,6 @@
         exchange(0, 1)
 
     def prepare(stage):
-        with scope(f"geoarrive_{stage}"):
-            arrival(0, stage)
         with scope(f"geo_{stage}"):
             tiles_in = merged_tiles(0, stage)
             spread_out(tiles_in, near_geo, 4, stage)
@@ -537,7 +554,8 @@
         start_sums(0, [(residual, precond), (precond, image)])
     turned_image = operate(3, load_tile, turned)
     with scope("sum1wait"):
-        norm, curve = end_sums(0, 2)
+        first_total = end_sums(0)
+        norm, curve = (total_by(group < 3, first_total, index) for index in range(2))
     with scope("mid"):
         gamma = norm / curve
         dipoles = each(lambda k, d, p: d + gamma * p, dipoles, precond)
@@ -551,9 +569,18 @@
                 (precond, second_image),
             ],
         )
+    with scope("turn"):
+        dipoles, residual, precond, second, image, second_image = (
+            each(lambda k, value: as_rows(value), vector)
+            for vector in (dipoles, residual, precond, second, image, second_image)
+        )
+        norm, curve = (total_by(row < 3, first_total, index) for index in range(2))
     with scope("sum2wait"):
-        norm_next, second_curve, cross, cross_back = end_sums(1, 4)
+        last_total = end_sums(1)
     with scope("out"):
+        norm_next, second_curve, cross, cross_back = (
+            total_by(row < 3, last_total, index) for index in range(4)
+        )
         ratio = norm_next / norm
         gamma = norm_next / (second_curve + ratio * (cross + cross_back + ratio * curve))
         for k in range(deep):
@@ -564,14 +591,11 @@
                 (res_out, residual[k] - gamma * along),
             ):
                 for part in range(6):
-                    turned_part = gather(value, GROUP * part + site)
-                    line = jnp.where(group == row, turned_part, 0.0)
-                    out[6 * k + part] = jnp.sum(line, axis=0, keepdims=True)
+                    out[6 * k + part] = value[part : part + 1]
     with scope("sendwait"):
-        for phase in range(4):
-            wait_all(phase, send_sems)
-        for number in range(2):
-            wait_sums(number, sum_send)
+        pltpu.make_async_copy(held, held, send_sem).wait()
+        rows = sums_in.at[:, pl.ds(0, total_devices - 1)]
+        pltpu.make_async_copy(rows, rows, sum_send).wait()
 
 
 def store(dipoles, residual, dip_out, res_out, sems):
@@ -608,9 +632,7 @@
         scratch_shapes=[
             pltpu.SMEM((deep, 1, pair_list.shape[-1]), jnp.int32),
             pltpu.SMEM((deep,), jnp.int32),
-            buffer(3 * deep, 1, slots),
-            buffer(deep, 1, slots),
-            buffer(6 * deep, 1, slots),
+            buffer(10 * deep, 1, slots),
             buffer(4, deep + 2 * tiles + 3, 8, slots),
             buffer(4, counts[0] + 2 * counts[1], 8, slots),
             buffer(PAGES, 6, rows + 16, slots),
@@ -620,10 +642,10 @@
             buffer(PAGES * SPAN * deep, 6, 8, slots),
             buffer(2, 1, slots),
             buffer(2, devices, 1, slots),
-            dma((5,)),
-            dma((4,)),
-            dma((4, 3)),
-            dma((2,)),
+            dma,
+            dma,
+            dma((3, 3)),
+            dma,
             dma((2,)),
         ],
         compiler_params=pltpu.CompilerParams(collective_id=0, has_side_effects=True),

time: 31.6 us -> 31.1 us (0.984)
  Pallas kernels: 30.8 us -> 30.3 us
    pallas_call x1, Pallas kernels: 30.2 us -> 29.7 us  [on_device(): pl.pallas_call(functools.partial(kernel, sizes, deep), out_shape=(line, l...]
where the time goes in v5:
time: 31.1 us; the launch traced here: 30.9 us
  Pallas kernels  30.3 us (97%)
  between operations  0.64 us (2%)
    pallas_call x1, Pallas kernels, on_device(): pl.pallas_call(functools.partial(kernel, sizes, deep), out_shape=(line, l...  29.7 us
    pallas_call x1, Pallas kernels, on_device(): pl.pallas_call(store, out_shape=(result, result), in_specs=[vmem, vmem],...  0.62 us

profile of v5, /device:TPU:0, one launch (start us, length us, event | category | flops | bytes accessed | tf_op | source)
XLA Modules:
  0.0 30.9 jit_solution(14978884927793428256)
XLA Ops:
  0.6 29.7 %shard_map.68 = (f32[18,1,128]{2,1,0:T(1,128)S(1)}, f32[18,1,128]{2,1,0:T(1,128)S(1)}) custom-call(s32[3,1,13]{2,1,0:T(1,128)} %bitcast.13, s32[3]{0:T(128)} %bitcast.15, f32[9,1,128]{2,1,0:T(1,128)} %bitcast.12, f32[3,1,128]{2,1,0:T(1,128)} %bitcast.14, f32[18,1,128]{2,1,0:T(1,128)} %bitcast.11), custom_call_target="tpu_custom_call" | custom-call | tf_op jit(solution)/shard_map/pallas_call | solution.py:627
  30.3 0.6 %shard_map.69 = (f32[18,1,128]{2,1,0:T(1,128)}, f32[18,1,128]{2,1,0:T(1,128)}) custom-call(f32[18,1,128]{2,1,0:T(1,128)S(1)} %get-tuple-element.6.dipoles, f32[18,1,128]{2,1,0:T(1,128)S(1)} %get-tuple-element.7.residual), custom_call_target="tpu_custom_call" | custom-call | tf_op jit(solution)/shard_map/pallas_call | solution.py:659

commit v6 on v5

--- a/solution.py
+++ b/solution.py
@@ -1,4 +1,5 @@
 import functools
+import math
 
 import jax
 import jax.numpy as jnp
@@ -20,6 +21,7 @@
 SPAN = 2 * REACH + 1
 ORDER = [(2, -1), (2, 1), (1, -1), (1, 1), (2, 0), (0, -1), (0, 1), (1, 0), (0, 0)]
 COLUMNS = [(cx, cy) for cx in (-1, 0, 1) for cy in (-1, 0, 1)]
+REST = 6
 EDGE = 12
 OWN = (0, 48)
 LOW = ((48, 60, 72), (36, 96, 108))
@@ -188,17 +190,32 @@
     SENT = {0: 0, 1: deep + 1, -1: deep + 2 + tiles}
     HALO = {0: deep, 1: deep + 1 + tiles, -1: deep + 2 + 2 * tiles}
 
+    sent_tiles = deep + 2 * tiles + 3
+    held_tiles = counts[0] + 2 * counts[1]
+
+    def sent_rows(phase, tile, amount=8):
+        return pl.ds(8 * (phase * sent_tiles + tile), amount)
+
+    def held_rows(phase, tile, amount=8):
+        return pl.ds(pl.multiple_of(8 * (phase * held_tiles + tile), 8), amount)
+
+    def put_tile(phase, tile, value):
+        send[sent_rows(phase, tile), :] = value
+
+    def ends(bottom, top):
+        return jnp.where(row < REACH, bottom, pltpu.roll(top, REST, 0))
+
     def put(phase, blocks):
         last = deep - 1
         for k in range(deep):
-            send[phase, MIDDLE + k] = blocks[k]
-        send[phase, HALO[0]] = jnp.where(row < 4, blocks[0], blocks[last])
+            put_tile(phase, MIDDLE + k, blocks[k])
+        put_tile(phase, HALO[0], ends(blocks[0], blocks[last]))
         for direction, take, ride, ride_at in (
             (1, take_low, ride_low, RIDE_LOW),
             (-1, take_high, ride_high, RIDE_HIGH),
         ):
             cut = {k: gather(blocks[k], take) for k in range(deep) if k not in riders or k == last}
-            send[phase, HALO[direction]] = jnp.where(row < 4, cut[0], cut[last])
+            put_tile(phase, HALO[direction], ends(cut[0], cut[last]))
             for rider in riders:
                 for s in range(2):
                     host = rider - 2 + s
@@ -206,43 +223,41 @@
                         within(ride_at, 3 * EDGE), gather(blocks[rider], ride[s]), cut[host]
                     )
             for k in tile_of:
-                send[phase, SENT[direction] + tile_of[k]] = cut[k]
+                put_tile(phase, SENT[direction] + tile_of[k], cut[k])
 
     def exchange(*phases):
-        def start(phase, src, at, stage, amount, target):
+        def start(phase, src, at, stage, rows, target):
             place = counts[0] + counts[1] * (1 - side_is_up[stage]) if stage else 0
             pltpu.make_async_remote_copy(
-                src_ref=send.at[phase, pl.ds(src, amount)],
-                dst_ref=held.at[phase, pl.ds(place + at, amount)],
+                src_ref=send.at[sent_rows(phase, src, rows)],
+                dst_ref=held.at[held_rows(phase, place + at, rows)],
                 send_sem=send_sem,
-                recv_sem=recv_sems.at[max(phase - 1, 0), 1 - side_sign[stage] if stage else 1],
+                recv_sem=recv_sems.at[phase, 1 - side_sign[stage] if stage else 1],
                 device_id=target,
                 device_id_type=MESH,
             ).start()
 
-        for stage, cx in ORDER:
-            cy = side_sign[stage] if stage else 0
-            far = 1 if stage else 0
-            for phase in phases:
+        for phase in phases:
+            for stage, cx in ORDER:
+                cy = side_sign[stage] if stage else 0
+                far = 1 if stage else 0
                 if stage or cx:
-                    amount = tiles if cx else deep
-                    start(
-                        phase, SENT[cx], inner[-cx, far], stage, amount, neighbour(cx, cy, 0)
-                    )
+                    rows = 8 * (tiles if cx else deep)
+                    start(phase, SENT[cx], inner[-cx, far], stage, rows, neighbour(cx, cy, 0))
                 for ring in range(rings):
                     at = halos[-cx, far] + ring
                     target = neighbour(cx, cy, -1 if ring == 0 else 1)
-                    start(phase, HALO[cx], at, stage, 1, target)
+                    start(phase, HALO[cx], at, stage, REST, target)
 
     def first_tile(stage):
         return counts[0] + counts[1] * side_is_up[stage] if stage else 0
 
+    rows_in = [8 * counts[far] - (8 - REST) * 3 * rings for far in (0, 1)]
+
     def arrival(phase, stage):
-        number = max(phase - 1, 0)
-        first = pl.ds(0, 2) if number == 0 else pl.ds(phase, 1)
-        rows = held.at[first, pl.ds(first_tile(stage), counts[1 if stage else 0])]
+        rows = held.at[held_rows(phase, first_tile(stage), rows_in[1 if stage else 0])]
         which = 1 + side_sign[stage] if stage else 1
-        pltpu.make_async_copy(rows, rows, recv_sems.at[number, which]).wait()
+        pltpu.make_async_copy(rows, rows, recv_sems.at[phase, which]).wait()
 
     def merged_tiles(phase, stage):
         first = first_tile(stage)
@@ -250,12 +265,11 @@
 
         def halo(cx):
             at = first + halos[cx, far]
-            if rings == 1:
-                return held[phase, at]
-            return jnp.where(row < 4, held[phase, at], held[phase, at + 1])
+            top = held[held_rows(phase, at + rings - 1), :]
+            return jnp.where(row < 4, held[held_rows(phase, at), :], pltpu.roll(top, 8 - REST, 0))
 
         def tile(cx, number):
-            return held[phase, first + inner[cx, far] + number]
+            return held[held_rows(phase, first + inner[cx, far] + number), :]
 
         both = []
         for s in range(2):
@@ -265,7 +279,7 @@
                 if v == 0:
                     low, own, high = halo(-1), halo(0), halo(1)
                 else:
-                    own = tile(0, k) if stage else send[phase, MIDDLE + k]
+                    own = tile(0, k) if stage else send[sent_rows(phase, MIDDLE + k), :]
                     if k in riders:
                         host = tile_of[k - 2 + s]
                         low = gather(tile(-1, host), leave_low)
@@ -300,12 +314,14 @@
                         out[page, part, pl.ds(8 * (deep + 1), 8), :] = value
 
     def contract(sums, parts, vec):
-        xx, yy, zz, xy, xz, yz = parts
+        dx, dy, dz, tx, ty, tz, three = parts
         for first in (0, 3):
             vx, vy, vz = vec[first : first + 3]
-            sums[first] = sums[first] + (xx * vx + xy * vy + xz * vz)
-            sums[first + 1] = sums[first + 1] + (xy * vx + yy * vy + yz * vz)
-            sums[first + 2] = sums[first + 2] + (xz * vx + yz * vy + zz * vz)
+            along = tx * vx + ty * vy + tz * vz
+            for part, (d, v) in enumerate(((dx, vx), (dy, vy), (dz, vz))):
+                term = d * along - three * v
+                at = first + part
+                sums[at] = term if sums[at] is None else sums[at] + term
 
     def tile_number(k, page, sz):
         return (k * PAGES + page) * SPAN + sz + REACH
@@ -319,23 +335,24 @@
         weight = switch[k, page, pl.ds(start, 8), :]
         if page == 0 and sz == 0:
             weight = jnp.where(group == REACH, 0.0, weight)
-        square = jnp.maximum(dx * dx + dy * dy + dz * dz, 1.0)
+        square = dx * dx + dy * dy + dz * dz
+        if page == 0 and sz == 0:
+            square = jnp.maximum(square, 1.0)
         inverse = lax.rsqrt(square)
         inverse_square = inverse * inverse
-        damp = square * square * inverse * (near_geo[page, 3, span, :] * own_ref[page, k, 3])
-        damping = jnp.exp(-damp)
-        fade = jnp.maximum(1.0 - square * (1.0 / cutoff_square), 0.0)
+        damp = square * (square * inverse) * (near_geo[page, 3, span, :] * own_ref[page, k, 3])
+        damping = jnp.exp2(damp * (-1.0 / math.log(2.0)))
+        fade = jnp.maximum(cutoff_square - square, 0.0)
         scale = fade * fade * (inverse_square * inverse) * weight
-        three = scale * (1.0 - damping)
-        five = (1.0 - (1.0 + damp) * damping) * scale * (3.0 * inverse_square)
-        tx, ty, tz = five * dx, five * dy, five * dz
-        parts = (tx * dx - three, ty * dy - three, tz * dz - three, tx * dy, tx * dz, ty * dz)
-        for part in range(6):
-            tensor[tile_number(k, page, sz), part] = parts[part]
+        three = scale - scale * damping
+        five = (three - scale * (damp * damping)) * (3.0 * inverse_square)
+        parts = (dx, dy, dz, five * dx, five * dy, five * dz, three)
+        for part, value in enumerate(parts):
+            tensor[tile_number(k, page, sz), part] = value
         return parts
 
     def load_tile(k, page, sz):
-        return [tensor[tile_number(k, page, sz), part] for part in range(6)]
+        return [tensor[tile_number(k, page, sz), part] for part in range(7)]
 
     def back_roll(stage, j):
         return lax.rem(128 - SIDE * side_sign[stage] * j, 128) if stage else 0
@@ -366,31 +383,50 @@
         moved = jnp.where(upper, total[0], total[1])
         return kept + pltpu.roll(moved, 64, 1)
 
-    def add_stage(make_tile, totals, stage, k):
+    def used(stage):
         for j in range(1, REACH + 1) if stage else [0]:
-            sums = [jnp.zeros((8, 128), jnp.float32)] * 6
+            yield j, [sz for sz in SHIFTS if j < REACH or abs(sz) < REACH]
+
+    def stage_tiles(stage, k):
+        for j, shifts in used(stage):
+            for sz in shifts:
+                build_tile(k, page_of(stage, j), sz)
+
+    def stage_sums(make_tile, stage, k):
+        result = []
+        for j, shifts in used(stage):
+            sums = [None] * 6
             page = page_of(stage, j)
-            for sz in SHIFTS:
-                if j == REACH and abs(sz) == REACH:
-                    continue
+            for sz in shifts:
                 span = pl.ds(8 * k + 8 + sz, 8)
                 vec = [near[page, part, span, :] for part in range(6)]
                 contract(sums, make_tile(k, page, sz), vec)
-            totals[k] = gather_groups(sums, stage, j, totals[k])
+            result.append((sums, stage, j))
+        return result
 
     def operate(phase, make_tile, vector, prepare=None):
         totals = [(None, None)] * deep
+        waiting = [[] for _ in range(deep)]
         image = []
         for stage in range(3):
+            if prepare is not None:
+                prepare(stage)
+            if prepare is not None and stage == 2:
+                with scope("tiles"):
+                    for k in range(deep):
+                        stage_tiles(stage, k)
+                make_tile = load_tile
             with scope(f"arrive{phase}_{stage}"):
                 arrival(phase, stage)
-            if prepare is not None:
-                prepare(stage)
             with scope(f"stage{phase}_{stage}"):
                 spread_out(merged_tiles(phase, stage), near, 6, stage)
                 for k in range(deep):
-                    add_stage(make_tile, totals, stage, k)
+                    for item in waiting[k]:
+                        totals[k] = gather_groups(*item, totals[k])
+                    waiting[k] = stage_sums(make_tile, stage, k)
                     if stage == 2:
+                        for item in waiting[k]:
+                            totals[k] = gather_groups(*item, totals[k])
                         image.append(vector[k] / polar[k] - mask[k] * fold(totals[k]))
         return image
 
@@ -412,11 +448,11 @@
             for k in range(deep):
                 v = (k + 1 + cz) % (deep + 1)
                 there = gather(tiles_in[1][v], theirs)
-                here = gather(send[0, MIDDLE + k], ours)
+                here = gather(send[sent_rows(0, MIDDLE + k), :], ours)
                 value = jnp.where(use_own, here, there)
                 if stage == 0 and cz == 0:
                     inside_own = jnp.logical_and(reached >= 0, reached < SIDE)
-                    value = jnp.where(inside_own, 1.0, value)
+                    value = jnp.where(inside_own, 1.0 / cutoff_square**2, value)
                 value = jnp.where(group < SPAN, value, 0.0)
                 span = pl.ds(8 * (cz + 1), 8)
                 if stage == 0:
@@ -437,7 +473,7 @@
 
     in_set = [group < 3, jnp.logical_and(group >= 3, group < 6)]
 
-    def start_sums(number, products):
+    def put_sums(number, products):
         values = []
         for first, second in products:
             value = first[0] * second[0]
@@ -452,6 +488,8 @@
             line = jnp.where(group[0:1] == index, values[index], line)
         sums_out[number] = line
         sums_in[number, my_id] = line
+
+    def send_sums(number):
         for target in everyone:
             pltpu.make_async_remote_copy(
                 src_ref=sums_out.at[number],
@@ -508,7 +546,7 @@
             flag = pairs_ref[k, 0, 0] == slot
             for entry in range(1, 13):
                 flag = jnp.logical_or(flag, pairs_ref[k, 0, entry] == slot)
-            flags = jnp.where(flag, 1.0, 0.0)
+            flags = jnp.where(flag, 1.0 / cutoff_square**2, 0.0)
             geometry.append(packed(places + [root, flags]))
             for stage in range(3):
                 for j in range(1, REACH + 1) if stage else [0]:
@@ -532,6 +570,8 @@
         exchange(0, 1)
 
     def prepare(stage):
+        with scope(f"geoarrive_{stage}"):
+            arrival(0, stage)
         with scope(f"geo_{stage}"):
             tiles_in = merged_tiles(0, stage)
             spread_out(tiles_in, near_geo, 4, stage)
@@ -548,10 +588,10 @@
     with scope("finish1"):
         turned = each(lambda k, q: polar[k] * q, image)
         put(3, each(lambda k, t: t * mask[k], turned))
+        put_sums(0, [(residual, precond), (precond, image)])
     with scope("send2"):
         exchange(3)
-    with scope("sum1"):
-        start_sums(0, [(residual, precond), (precond, image)])
+        send_sums(0)
     turned_image = operate(3, load_tile, turned)
     with scope("sum1wait"):
         first_total = end_sums(0)
@@ -562,13 +602,14 @@
         residual = each(lambda k, r, q: r - gamma * q, residual, image)
         second = each(lambda k, r: polar[k] * r, residual)
         second_image = each(lambda k, q, t: q - gamma * t, image, turned_image)
-        start_sums(
+        put_sums(
             1,
             [
                 (residual, second), (second, second_image), (second, image),
                 (precond, second_image),
             ],
         )
+        send_sums(1)
     with scope("turn"):
         dipoles, residual, precond, second, image, second_image = (
             each(lambda k, value: as_rows(value), vector)
@@ -593,7 +634,8 @@
                 for part in range(6):
                     out[6 * k + part] = value[part : part + 1]
     with scope("sendwait"):
-        pltpu.make_async_copy(held, held, send_sem).wait()
+        rows = held.at[pl.ds(0, 4 * (rows_in[0] + 2 * rows_in[1]))]
+        pltpu.make_async_copy(rows, rows, send_sem).wait()
         rows = sums_in.at[:, pl.ds(0, total_devices - 1)]
         pltpu.make_async_copy(rows, rows, sum_send).wait()
 
@@ -633,18 +675,18 @@
             pltpu.SMEM((deep, 1, pair_list.shape[-1]), jnp.int32),
             pltpu.SMEM((deep,), jnp.int32),
             buffer(10 * deep, 1, slots),
-            buffer(4, deep + 2 * tiles + 3, 8, slots),
-            buffer(4, counts[0] + 2 * counts[1], 8, slots),
+            buffer(4 * 8 * (deep + 2 * tiles + 3), slots),
+            buffer(4 * 8 * (counts[0] + 2 * counts[1]), slots),
             buffer(PAGES, 6, rows + 16, slots),
             buffer(PAGES, 4, rows + 16, slots),
             buffer(PAGES, deep, 4, 8, slots),
             buffer(deep, PAGES, 24, slots),
-            buffer(PAGES * SPAN * deep, 6, 8, slots),
+            buffer(PAGES * SPAN * deep, 7, 8, slots),
             buffer(2, 1, slots),
             buffer(2, devices, 1, slots),
             dma,
             dma,
-            dma((3, 3)),
+            dma((4, 3)),
             dma,
             dma((2,)),
         ],

time: 31.1 us -> 31.1 us (level)
  no operation moved by 1% of the time
where the time goes in v6:
time: 31.1 us; the launch traced here: 30.9 us
  Pallas kernels  30.3 us (97%)
  between operations  0.64 us (2%)
    pallas_call x1, Pallas kernels, on_device(): pl.pallas_call(functools.partial(kernel, sizes, deep), out_shape=(line, l...  29.7 us
    pallas_call x1, Pallas kernels, on_device(): pl.pallas_call(store, out_shape=(result, result), in_specs=[vmem, vmem],...  0.62 us

profile of v6, /device:TPU:0, one launch (start us, length us, event | category | flops | bytes accessed | tf_op | source)
XLA Modules:
  0.0 30.9 jit_solution(16512601974725266107)
XLA Ops:
  0.6 29.7 %shard_map.68 = (f32[18,1,128]{2,1,0:T(1,128)S(1)}, f32[18,1,128]{2,1,0:T(1,128)S(1)}) custom-call(s32[3,1,13]{2,1,0:T(1,128)} %bitcast.13, s32[3]{0:T(128)} %bitcast.15, f32[9,1,128]{2,1,0:T(1,128)} %bitcast.12, f32[3,1,128]{2,1,0:T(1,128)} %bitcast.14, f32[18,1,128]{2,1,0:T(1,128)} %bitcast.11), custom_call_target="tpu_custom_call" | custom-call | tf_op jit(solution)/shard_map/pallas_call | solution.py:669
  30.3 0.6 %shard_map.69 = (f32[18,1,128]{2,1,0:T(1,128)}, f32[18,1,128]{2,1,0:T(1,128)}) custom-call(f32[18,1,128]{2,1,0:T(1,128)S(1)} %get-tuple-element.6.dipoles, f32[18,1,128]{2,1,0:T(1,128)S(1)} %get-tuple-element.7.residual), custom_call_target="tpu_custom_call" | custom-call | tf_op jit(solution)/shard_map/pallas_call | solution.py:701

commit v7 on v6

--- a/solution.py
+++ b/solution.py
@@ -28,6 +28,9 @@
 HIGH = ((84, 96, 108), (0, 12, 24))
 RIDE_LOW = 0
 RIDE_HIGH = 36
+WIDE_LOW = (84, 0)
+WIDE_HIGH = (48, 12)
+WIDE_FLAGS = 120
 FLAGS = 4
 
 
@@ -58,7 +61,7 @@
 
 def kernel(
     sizes, deep, pairs_hbm, count_hbm, coords_hbm, polar_hbm, field_hbm, dip_out, res_out,
-    pairs_ref, count_ref, lines, send, held, near, near_geo, own_ref,
+    pairs_ref, count_ref, lines, send, held, send_wide, held_wide, near, near_geo, own_ref,
     switch, tensor, sums_out, sums_in, load_sem, send_sem, recv_sems, sum_send, sum_recv,
 ):
     total_devices = sizes[0] * sizes[1] * sizes[2]
@@ -149,15 +152,25 @@
         for s in range(2)
     ]
 
-    def unride(regions, start):
+    def unride(regions, starts):
         cases = []
-        for bases in regions:
+        for bases, start in zip(regions, starts):
             for part, base in enumerate(bases):
                 cases.append((within(base, EDGE), lane - base + start + EDGE * part))
         return choose(cases, jnp.zeros_like(lane))
 
-    leave_low = unride(LOW, RIDE_LOW)
-    leave_high = unride(HIGH, RIDE_HIGH)
+    leave_low = unride(LOW, (RIDE_LOW, RIDE_LOW))
+    leave_high = unride(HIGH, (RIDE_HIGH, RIDE_HIGH))
+    part_low = unride(LOW, WIDE_LOW)
+    part_high = unride(HIGH, WIDE_HIGH)
+    wide_low, wide_high = (
+        edge_index([at + EDGE * part for at in starts for part in range(3)], all_parts, first_x)
+        for starts, first_x in ((WIDE_LOW, 1), (WIDE_HIGH, 0))
+    )
+    has_ninth = jnp.logical_or(row == 1, row == 7)
+    flag = jnp.where(has_ninth, 8, jnp.maximum(lane - WIDE_FLAGS, 0))
+    flag_lane = OWN[1] + GROUP * (FLAGS - 3) + SIDE * (flag // 3) + 1 + flag % 3
+    take_wide_low = jnp.where(lane >= WIDE_FLAGS, flag_lane, take_low)
 
     def inside(bases, size):
         result = within(bases[0], size)
@@ -205,11 +218,28 @@
     def ends(bottom, top):
         return jnp.where(row < REACH, bottom, pltpu.roll(top, REST, 0))
 
+    def put_first(geometry, vector):
+        for phase, blocks in ((0, geometry), (1, vector)):
+            put_middle(phase, blocks)
+        for place, take, part, is_part in (
+            (0, take_wide_low, wide_low, inside((0, 84), 3 * EDGE)),
+            (deep + 1, take_high, wide_high, within(12, 6 * EDGE)),
+        ):
+            cut = [
+                jnp.where(is_part, gather(vector[k], part), gather(geometry[k], take))
+                for k in range(deep)
+            ]
+            for index, value in enumerate(cut + [ends(cut[0], cut[-1])]):
+                send_wide[pl.ds(8 * (place + index), 8), :] = value
+
+    def put_middle(phase, blocks):
+        for k in range(deep):
+            put_tile(phase, MIDDLE + k, blocks[k])
+        put_tile(phase, HALO[0], ends(blocks[0], blocks[deep - 1]))
+
     def put(phase, blocks):
         last = deep - 1
-        for k in range(deep):
-            put_tile(phase, MIDDLE + k, blocks[k])
-        put_tile(phase, HALO[0], ends(blocks[0], blocks[last]))
+        put_middle(phase, blocks)
         for direction, take, ride, ride_at in (
             (1, take_low, ride_low, RIDE_LOW),
             (-1, take_high, ride_high, RIDE_HIGH),
@@ -249,15 +279,98 @@
                     target = neighbour(cx, cy, -1 if ring == 0 else 1)
                     start(phase, HALO[cx], at, stage, REST, target)
 
+    wide_count = 2 * (deep + rings)
+
+    def first_wide(stage):
+        return wide_count * (1 + side_is_up[stage]) if stage else 0
+
+    def wide_place(cx, ring=None):
+        right = 1 if cx > 0 else 0
+        return right * deep if ring is None else 2 * deep + right * rings + ring
+
+    def wide_rows(stage, place, amount=8):
+        return pl.ds(pl.multiple_of(8 * (first_wide(stage) + place), 8), amount)
+
+    def exchange_first():
+        def start(phase, src, dst, stage, target):
+            pltpu.make_async_remote_copy(
+                src_ref=src,
+                dst_ref=dst,
+                send_sem=send_sem,
+                recv_sem=recv_sems.at[phase, 1 - side_sign[stage] if stage else 1],
+                device_id=target,
+                device_id_type=MESH,
+            ).start()
+
+        for phase in range(2):
+            for stage, cx in ORDER:
+                cy = side_sign[stage] if stage else 0
+                far = 1 if stage else 0
+                opposite = 3 - stage if stage else 0
+                rows = 8 * deep
+                if cx and phase == 0:
+                    place = 0 if cx > 0 else deep + 1
+                    start(
+                        0,
+                        send_wide.at[pl.ds(8 * place, rows)],
+                        held_wide.at[wide_rows(opposite, wide_place(-cx), rows)],
+                        stage,
+                        neighbour(cx, cy, 0),
+                    )
+                    for ring in range(rings):
+                        start(
+                            0,
+                            send_wide.at[pl.ds(8 * (place + deep), REST)],
+                            held_wide.at[wide_rows(opposite, wide_place(-cx, ring), REST)],
+                            stage,
+                            neighbour(cx, cy, -1 if ring == 0 else 1),
+                        )
+                if not cx:
+                    first = first_tile(opposite)
+                    if stage:
+                        start(
+                            phase,
+                            send.at[sent_rows(phase, SENT[0], rows)],
+                            held.at[held_rows(phase, first + inner[0, far], rows)],
+                            stage,
+                            neighbour(0, cy, 0),
+                        )
+                    for ring in range(rings):
+                        start(
+                            phase,
+                            send.at[sent_rows(phase, HALO[0], REST)],
+                            held.at[held_rows(phase, first + halos[0, far] + ring, REST)],
+                            stage,
+                            neighbour(0, cy, -1 if ring == 0 else 1),
+                        )
+
     def first_tile(stage):
         return counts[0] + counts[1] * side_is_up[stage] if stage else 0
 
-    rows_in = [8 * counts[far] - (8 - REST) * 3 * rings for far in (0, 1)]
+    rows_in = []
+    for phase in range(4):
+        if phase < 2:
+            sides = 2 * (8 * deep + REST * rings) if phase == 0 else 0
+            rows_in.append([sides + REST * rings, sides + REST * rings + 8 * deep])
+        else:
+            rows_in.append([8 * counts[far] - (8 - REST) * 3 * rings for far in (0, 1)])
 
     def arrival(phase, stage):
-        rows = held.at[held_rows(phase, first_tile(stage), rows_in[1 if stage else 0])]
+        start = first_tile(stage) if phase > 1 else 0
+        rows = held.at[held_rows(phase, start, rows_in[phase][1 if stage else 0])]
         which = 1 + side_sign[stage] if stage else 1
         pltpu.make_async_copy(rows, rows, recv_sems.at[phase, which]).wait()
+
+    def joined(below, above):
+        return jnp.where(row < 4, below, pltpu.roll(above, 8 - REST, 0))
+
+    def wide_tile(stage, cx, v):
+        if v:
+            return held_wide[wide_rows(stage, wide_place(cx) + v - 1), :]
+        return joined(
+            held_wide[wide_rows(stage, wide_place(cx, 0)), :],
+            held_wide[wide_rows(stage, wide_place(cx, rings - 1)), :],
+        )
 
     def merged_tiles(phase, stage):
         first = first_tile(stage)
@@ -265,18 +378,31 @@
 
         def halo(cx):
             at = first + halos[cx, far]
-            top = held[held_rows(phase, at + rings - 1), :]
-            return jnp.where(row < 4, held[held_rows(phase, at), :], pltpu.roll(top, 8 - REST, 0))
+            return joined(
+                held[held_rows(phase, at), :], held[held_rows(phase, at + rings - 1), :]
+            )
 
         def tile(cx, number):
             return held[held_rows(phase, first + inner[cx, far] + number), :]
 
+        wide = []
+        for v in range(deep + 1) if phase < 2 else []:
+            low, high = wide_tile(stage, -1, v), wide_tile(stage, 1, v)
+            if phase == 1:
+                low, high = gather(low, part_low), gather(high, part_high)
+            wide.append((low, high))
         both = []
         for s in range(2):
             row_of_tiles = []
             for v in range(deep + 1):
                 k = v - 1
-                if v == 0:
+                if wide:
+                    low, high = wide[v]
+                    if v == 0:
+                        own = halo(0)
+                    else:
+                        own = tile(0, k) if stage else send[sent_rows(phase, MIDDLE + k), :]
+                elif v == 0:
                     low, own, high = halo(-1), halo(0), halo(1)
                 else:
                     own = tile(0, k) if stage else send[sent_rows(phase, MIDDLE + k), :]
@@ -435,19 +561,30 @@
             return jnp.broadcast_to(jnp.asarray(at, jnp.int32), (8, 128))
 
         own_lane = OWN[1] + GROUP * (FLAGS - 3)
-        low_lane = LOW[1][FLAGS - 3]
+
+        def same_rows(tile, low_row, high_row):
+            return jnp.where(row < 4, tile[low_row : low_row + 1], tile[high_row : high_row + 1])
+
         cy = side_sign[stage] if stage else 0
         for cz in (-1, 0, 1):
-            low_at = full(low_lane + 7 - 3 * (cy + 1) - cz)
+            low_flag = 7 - 3 * (cy + 1) - cz
+            ninth = low_flag == 8 if stage and cz == -1 else None
+            low_at = low_flag if ninth is None else jnp.where(ninth, 0, low_flag)
+            low_at = full(WIDE_FLAGS + low_at)
             high_at = full(own_lane + SIDE * (cy + 1) + cz + 2)
             middle_at = full(own_lane + SIDE * (2 + cy * cz) if stage else own_lane)
-            theirs = jnp.where(reached < 0, low_at, middle_at)
             ours = jnp.where(reached < SIDE, middle_at, high_at)
             ahead = cy > 0 if stage else cz > 0
             use_own = jnp.where(ahead, reached, reached - SIDE) >= 0
             for k in range(deep):
                 v = (k + 1 + cz) % (deep + 1)
-                there = gather(tiles_in[1][v], theirs)
+                tile = wide_tile(stage, -1, v)
+                flags = same_rows(tile, 0, 6)
+                if ninth is not None:
+                    flags = jnp.where(ninth, same_rows(tile, 1, 7), flags)
+                there = jnp.where(
+                    reached < 0, gather(flags, low_at), gather(tiles_in[1][v], middle_at)
+                )
                 here = gather(send[sent_rows(0, MIDDLE + k), :], ours)
                 value = jnp.where(use_own, here, there)
                 if stage == 0 and cz == 0:
@@ -562,12 +699,11 @@
             field_k = packed([rows_of(field_ref[6 * k + part]) for part in range(6)])
             source.append(field_k * mask_k)
         dipoles = each(lambda k, s: polar[k] * s, source)
-        put(0, geometry)
-        put(1, each(lambda k, d: d * mask[k], dipoles))
+        put_first(geometry, each(lambda k, d: d * mask[k], dipoles))
     with scope("barrier"):
         pl.semaphore_wait(barrier, len(greeted))
     with scope("send0"):
-        exchange(0, 1)
+        exchange_first()
 
     def prepare(stage):
         with scope(f"geoarrive_{stage}"):
@@ -634,7 +770,7 @@
                 for part in range(6):
                     out[6 * k + part] = value[part : part + 1]
     with scope("sendwait"):
-        rows = held.at[pl.ds(0, 4 * (rows_in[0] + 2 * rows_in[1]))]
+        rows = held.at[pl.ds(0, sum(middle + 2 * side for middle, side in rows_in))]
         pltpu.make_async_copy(rows, rows, send_sem).wait()
         rows = sums_in.at[:, pl.ds(0, total_devices - 1)]
         pltpu.make_async_copy(rows, rows, sum_send).wait()
@@ -658,7 +794,8 @@
     hbm = pl.BlockSpec(memory_space=pl.ANY)
     rows = 8 * deep
     devices = sizes[0] * sizes[1] * sizes[2]
-    tiles, counts = (plan(deep, 1 if sizes[2] == 2 else 2)[index] for index in (2, 5))
+    rings = 1 if sizes[2] == 2 else 2
+    tiles, counts = (plan(deep, rings)[index] for index in (2, 5))
 
     def buffer(*shape):
         return pltpu.VMEM(shape, jnp.float32)
@@ -677,6 +814,8 @@
             buffer(10 * deep, 1, slots),
             buffer(4 * 8 * (deep + 2 * tiles + 3), slots),
             buffer(4 * 8 * (counts[0] + 2 * counts[1]), slots),
+            buffer(8 * 2 * (deep + 1), slots),
+            buffer(8 * 3 * 2 * (deep + rings), slots),
             buffer(PAGES, 6, rows + 16, slots),
             buffer(PAGES, 4, rows + 16, slots),
             buffer(PAGES, deep, 4, 8, slots),

time: 31.1 us -> 30 us (0.965)
  Pallas kernels: 30.3 us -> 29.2 us
    pallas_call x1, Pallas kernels: 29.7 us -> 28.6 us  [on_device(): pl.pallas_call(functools.partial(kernel, sizes, deep), out_shape=(line, l...]
where the time goes in v7:
time: 30 us; the launch traced here: 29.9 us
  Pallas kernels  29.2 us (97%)
  between operations  0.64 us (2%)
    pallas_call x1, Pallas kernels, on_device(): pl.pallas_call(functools.partial(kernel, sizes, deep), out_shape=(line, l...  28.6 us
    pallas_call x1, Pallas kernels, on_device(): pl.pallas_call(store, out_shape=(result, result), in_specs=[vmem, vmem],...  0.62 us

profile of v7, /device:TPU:0, one launch (start us, length us, event | category | flops | bytes accessed | tf_op | source)
XLA Modules:
  0.0 29.9 jit_solution(346810261319595700)
XLA Ops:
  0.6 28.6 %shard_map.68 = (f32[18,1,128]{2,1,0:T(1,128)S(1)}, f32[18,1,128]{2,1,0:T(1,128)S(1)}) custom-call(s32[3,1,13]{2,1,0:T(1,128)} %bitcast.13, s32[3]{0:T(128)} %bitcast.15, f32[9,1,128]{2,1,0:T(1,128)} %bitcast.12, f32[3,1,128]{2,1,0:T(1,128)} %bitcast.14, f32[18,1,128]{2,1,0:T(1,128)} %bitcast.11), custom_call_target="tpu_custom_call" | custom-call | tf_op jit(solution)/shard_map/pallas_call | solution.py:806
  29.2 0.6 %shard_map.69 = (f32[18,1,128]{2,1,0:T(1,128)}, f32[18,1,128]{2,1,0:T(1,128)}) custom-call(f32[18,1,128]{2,1,0:T(1,128)S(1)} %get-tuple-element.6.dipoles, f32[18,1,128]{2,1,0:T(1,128)S(1)} %get-tuple-element.7.residual), custom_call_target="tpu_custom_call" | custom-call | tf_op jit(solution)/shard_map/pallas_call | solution.py:840

commit v8 on v7

--- a/solution.py
+++ b/solution.py
@@ -255,7 +255,7 @@
             for k in tile_of:
                 put_tile(phase, SENT[direction] + tile_of[k], cut[k])
 
-    def exchange(*phases):
+    def exchange(phase, between=None):
         def start(phase, src, at, stage, rows, target):
             place = counts[0] + counts[1] * (1 - side_is_up[stage]) if stage else 0
             pltpu.make_async_remote_copy(
@@ -267,17 +267,18 @@
                 device_id_type=MESH,
             ).start()
 
-        for phase in phases:
-            for stage, cx in ORDER:
-                cy = side_sign[stage] if stage else 0
-                far = 1 if stage else 0
-                if stage or cx:
-                    rows = 8 * (tiles if cx else deep)
-                    start(phase, SENT[cx], inner[-cx, far], stage, rows, neighbour(cx, cy, 0))
-                for ring in range(rings):
-                    at = halos[-cx, far] + ring
-                    target = neighbour(cx, cy, -1 if ring == 0 else 1)
-                    start(phase, HALO[cx], at, stage, REST, target)
+        for index, (stage, cx) in enumerate(ORDER):
+            if index == 2 and between is not None:
+                between()
+            cy = side_sign[stage] if stage else 0
+            far = 1 if stage else 0
+            if stage or cx:
+                rows = 8 * (tiles if cx else deep)
+                start(phase, SENT[cx], inner[-cx, far], stage, rows, neighbour(cx, cy, 0))
+            for ring in range(rings):
+                at = halos[-cx, far] + ring
+                target = neighbour(cx, cy, -1 if ring == 0 else 1)
+                start(phase, HALO[cx], at, stage, REST, target)
 
     wide_count = 2 * (deep + rings)
 
@@ -726,8 +727,7 @@
         put(3, each(lambda k, t: t * mask[k], turned))
         put_sums(0, [(residual, precond), (precond, image)])
     with scope("send2"):
-        exchange(3)
-        send_sums(0)
+        exchange(3, lambda: send_sums(0))
     turned_image = operate(3, load_tile, turned)
     with scope("sum1wait"):
         first_total = end_sums(0)

time: 30 us -> 29.7 us (0.990)
  Pallas kernels: 29.2 us -> 28.9 us
where the time goes in v8:
time: 29.7 us; the launch traced here: 29.6 us
  Pallas kernels  28.9 us (97%)
  between operations  0.64 us (2%)
    pallas_call x1, Pallas kernels, on_device(): pl.pallas_call(functools.partial(kernel, sizes, deep), out_shape=(line, l...  28.3 us
    pallas_call x1, Pallas kernels, on_device(): pl.pallas_call(store, out_shape=(result, result), in_specs=[vmem, vmem],...  0.62 us

profile of v8, /device:TPU:0, one launch (start us, length us, event | category | flops | bytes accessed | tf_op | source)
XLA Modules:
  0.0 29.6 jit_solution(4997916195668293089)
XLA Ops:
  0.6 28.3 %shard_map.68 = (f32[18,1,128]{2,1,0:T(1,128)S(1)}, f32[18,1,128]{2,1,0:T(1,128)S(1)}) custom-call(s32[3,1,13]{2,1,0:T(1,128)} %bitcast.13, s32[3]{0:T(128)} %bitcast.15, f32[9,1,128]{2,1,0:T(1,128)} %bitcast.12, f32[3,1,128]{2,1,0:T(1,128)} %bitcast.14, f32[18,1,128]{2,1,0:T(1,128)} %bitcast.11), custom_call_target="tpu_custom_call" | custom-call | tf_op jit(solution)/shard_map/pallas_call | solution.py:806
  29.0 0.6 %shard_map.69 = (f32[18,1,128]{2,1,0:T(1,128)}, f32[18,1,128]{2,1,0:T(1,128)}) custom-call(f32[18,1,128]{2,1,0:T(1,128)S(1)} %get-tuple-element.6.dipoles, f32[18,1,128]{2,1,0:T(1,128)S(1)} %get-tuple-element.7.residual), custom_call_target="tpu_custom_call" | custom-call | tf_op jit(solution)/shard_map/pallas_call | solution.py:840

commit v9 on v8

--- a/solution.py
+++ b/solution.py
@@ -19,7 +19,7 @@
 SHIFTS = range(-REACH, REACH + 1)
 PAGES = 1 + 2 * REACH
 SPAN = 2 * REACH + 1
-ORDER = [(2, -1), (2, 1), (1, -1), (1, 1), (2, 0), (0, -1), (0, 1), (1, 0), (0, 0)]
+ORDER = [(2, -1), (2, 1), (2, 0), (1, -1), (1, 1), (0, -1), (0, 1), (1, 0), (0, 0)]
 COLUMNS = [(cx, cy) for cx in (-1, 0, 1) for cy in (-1, 0, 1)]
 REST = 6
 EDGE = 12

time: 29.7 us -> 29.6 us (level)
  no operation moved by 1% of the time
where the time goes in v9:
time: 29.6 us; the launch traced here: 29.4 us
  Pallas kernels  28.8 us (97%)
  between operations  0.64 us (2%)
    pallas_call x1, Pallas kernels, on_device(): pl.pallas_call(functools.partial(kernel, sizes, deep), out_shape=(line, l...  28.2 us
    pallas_call x1, Pallas kernels, on_device(): pl.pallas_call(store, out_shape=(result, result), in_specs=[vmem, vmem],...  0.62 us

profile of v9, /device:TPU:0, one launch (start us, length us, event | category | flops | bytes accessed | tf_op | source)
XLA Modules:
  0.0 29.4 jit_solution(16716186700369672922)
XLA Ops:
  0.6 28.2 %shard_map.68 = (f32[18,1,128]{2,1,0:T(1,128)S(1)}, f32[18,1,128]{2,1,0:T(1,128)S(1)}) custom-call(s32[3,1,13]{2,1,0:T(1,128)} %bitcast.13, s32[3]{0:T(128)} %bitcast.15, f32[9,1,128]{2,1,0:T(1,128)} %bitcast.12, f32[3,1,128]{2,1,0:T(1,128)} %bitcast.14, f32[18,1,128]{2,1,0:T(1,128)} %bitcast.11), custom_call_target="tpu_custom_call" | custom-call | tf_op jit(solution)/shard_map/pallas_call | solution.py:806
  28.8 0.6 %shard_map.69 = (f32[18,1,128]{2,1,0:T(1,128)}, f32[18,1,128]{2,1,0:T(1,128)}) custom-call(f32[18,1,128]{2,1,0:T(1,128)S(1)} %get-tuple-element.6.dipoles, f32[18,1,128]{2,1,0:T(1,128)S(1)} %get-tuple-element.7.residual), custom_call_target="tpu_custom_call" | custom-call | tf_op jit(solution)/shard_map/pallas_call | solution.py:840
